TPU v7x, 128 devices: a whole 4x4x4 slice. The times are simulated.
128 devices in a mesh: aa: 32 (over y, z_hi, x), ba: 4 (over z_lo, core).
Axes of the slice: x: 4, y: 4, z: 4 (z_hi: 2, z_lo: 2; z = z_hi * 2 + z_lo), core: 2. Of those that a mesh axis runs over, the one named last changes fastest.
Arguments:
- fast_query: bfloat16 [2, 8192, 5120], P(None, 'aa', 'ba'), may hold values from -6 to 6
- fast_key: bfloat16 [2, 8192, 5120], P(None, 'aa', 'ba'), may hold values from -6 to 6
- fast_value: bfloat16 [2, 8192, 5120], P(None, 'aa', 'ba'), may hold values from -6 to 6
- rates: float32 [2, 8192, 24], P(None, 'aa', 'ba'), may hold values from 5e-05 to 0.0005
- attn_query: bfloat16 [2, 8192, 5120], P(None, 'aa', 'ba'), may hold values from -4.5 to 4.5
- attn_key: bfloat16 [2, 8192, 5120], P(None, 'aa', 'ba'), may hold values from -4.5 to 4.5
- attn_value: bfloat16 [2, 8192, 5120], P(None, 'aa', 'ba'), may hold values from -6 to 6
- fast_weights: float32 [640, 3, 8, 640], P('aa', None, 'ba'), may hold values from -0.2814427 to 0.2814427
- gain: float32 [5120], replicated, may hold values from 0.5 to 1.5
Outputs:
- mixed: bfloat16 [2, 8192, 5120], P(None, ('aa', 'ba'))
- weights_out: float32 [640, 3, 8, 640], P('aa', None, 'ba')
- moment_out: float32 [640, 3, 8, 640], P('aa', None, 'ba')
All inputs are finite; a program needn't handle non-finite values.
Results may differ from a plain program's by a relative error of at most 0.028.
Values may be sent and summed in bfloat16 or wider, within the bound.
No kernel may reach another device: no remote copies, remote signals or barrier semaphores. Data moves between devices by JAX's collectives and lax.ppermute only.
A program may use at most 192 MiB of HBM per device.

v0:
```python
import math

import jax
import jax.numpy as jnp
from jax import lax
from jax.sharding import Mesh
from jax.sharding import PartitionSpec as P

AD = 128
WINDOW = 512
AA = ("aa_0", "aa_1", "aa_2")
BA = ("ba_0", "ba_1")
AA_BA = ("aa_0", "aa_1", "aa_2", "ba_0", "ba_1")


BETA = 0.9
EPS = 1e-06


def own_block(pieces, axes, sequence):
    inside = pieces.shape[1:]
    pieces = pieces.reshape(*(lax.axis_size(a) for a in axes), *inside)
    pieces = jnp.moveaxis(pieces, sequence, range(len(axes))).reshape(-1, *inside)
    for k in sequence:
        pieces = lax.psum_scatter(pieces, axes[k], scatter_dimension=0, tiled=True)
    return pieces[0]


def split_up(shard, dim, length):
    before, after = (shard.shape[:dim], shard.shape[dim + 1 :])
    return jnp.moveaxis(shard.reshape(*before, length, -1, *after), dim, 0)


def scatter_axes(shard, axes, sequence, dim):
    length = lax.axis_size(axes)
    return own_block(split_up(shard, dim, length), axes, sequence)


def sent_to_all(shard, axis):
    copies = jnp.broadcast_to(shard, (lax.axis_size(axis), *shard.shape))
    return lax.all_to_all(copies, axis, split_axis=0, concat_axis=0, tiled=True)


def taken_together(shard, axis):
    return sent_to_all(shard, axis).sum(axis=0)


def from_behind(shard, axis, by):
    length = lax.axis_size(axis)
    return lax.ppermute(shard, axis, [(i, (i + by) % length) for i in range(length)])


def laid_out(pieces, dim):
    pieces = jnp.moveaxis(pieces, 0, dim)
    lengths = pieces.shape
    return pieces.reshape(*lengths[:dim], lengths[dim] * lengths[dim + 1], *lengths[dim + 2 :])


def turned_blocks(pieces, axes, sequence):
    lengths = [lax.axis_size(a) for a in axes]
    pieces = pieces.reshape(*lengths, *pieces.shape[1:])
    for k in sequence:
        pieces = lax.all_to_all(pieces, axes[k], split_axis=k, concat_axis=k, tiled=True)
    return pieces.reshape(-1, *pieces.shape[len(axes) :])


def exchange_by_chip(shard, groups, sequence, split_dim, concat_dim):
    length = lax.axis_size(groups[0]) * lax.axis_size(groups[1])
    pieces = split_up(shard, split_dim, length)
    return laid_out(turned_blocks(pieces, groups, sequence), concat_dim)


def activation(x):
    sig = jax.nn.sigmoid(x)
    return (x * sig, sig * (1.0 + x * (1.0 - sig)))


def project(x, w):
    return jnp.einsum("nhd,fhd->nhf", x, w, preferred_element_type=jnp.float32)


def fast_stretch(wfull, query, key, value, rate):
    rows = query.shape[0]
    heads = wfull.shape[2]
    depth = wfull.shape[3]
    q = query.reshape(rows, heads, depth)
    k = key.reshape(rows, heads, depth)
    v = value.reshape(rows, heads, depth)
    act_q, slope_q = activation(project(q, wfull[:, 0]))
    hidden_q = (act_q * project(q, wfull[:, 1])).astype(jnp.bfloat16)
    out = jnp.einsum(
        "nhf,fhd->nhd", hidden_q, wfull[:, 2], preferred_element_type=jnp.float32
    ).reshape(rows, heads * depth)
    gate_in = project(k, wfull[:, 0])
    up_in = project(k, wfull[:, 1])
    back_in = project(v, wfull[:, 2])
    act, slope = activation(gate_in)
    gate_x = (rate[..., 0:1] * (-back_in * up_in * slope)).astype(jnp.bfloat16)
    up_x = (rate[..., 1:2] * (-back_in * act)).astype(jnp.bfloat16)
    down_x = (rate[..., 2:3] * -(act * up_in)).astype(jnp.bfloat16)

    def term(start, count):

        def part(left, right):
            return jnp.einsum("nhf,nhd->fhd", left, right, preferred_element_type=jnp.float32)

        return jnp.stack([part(gate_x, k), part(up_x, k), part(down_x, v)], 1)

    return (out, term)


def reduce_rows(term, count):
    return scatter_axes(
        term(jnp.int32(0), count * lax.axis_size(AA)).astype(jnp.bfloat16), AA, (0, 2, 1), 0
    ).astype(jnp.float32)


def renorm(trial, target):
    squares = taken_together(jnp.sum(trial * trial, 0), AA)
    return trial * (target / jnp.sqrt(squares + EPS))


def local(
    fast_query, fast_key, fast_value, rates, attn_query, attn_key, attn_value, fast_weights, gain
):
    stretches, rows, width = fast_query.shape
    local_rows = fast_weights.shape[0]
    heads = fast_weights.shape[2]
    rate = rates.reshape(stretches, rows, heads, 3)
    index = lax.axis_index(AA)
    groups = lax.axis_size(AA)
    first_row = index * local_rows
    fast_out = []
    full = lax.all_gather(fast_weights.astype(jnp.bfloat16), AA, axis=0, tiled=True).astype(
        fast_weights.dtype
    )
    target = jnp.sqrt(jnp.sum(full * full, 0) + EPS)
    out, term = fast_stretch(
        full.astype(jnp.bfloat16), fast_query[0], fast_key[0], fast_value[0], rate[0]
    )
    fast_out.append(out)
    grads = lax.psum(term(0, full.shape[0]).astype(jnp.bfloat16), AA).astype(jnp.float32)
    trial = full - grads
    updated = trial * (target / jnp.sqrt(jnp.sum(trial * trial, 0) + EPS))
    out, term = fast_stretch(
        updated.astype(jnp.bfloat16), fast_query[1], fast_key[1], fast_value[1], rate[1]
    )
    fast_out.append(out)
    moment = BETA * lax.dynamic_slice_in_dim(grads, first_row, local_rows, 0) + reduce_rows(
        term, local_rows
    )
    own = lax.dynamic_slice_in_dim(updated, first_row, local_rows, 0)
    weights = renorm(own - moment, target)
    aheads = attn_query.shape[2] // AD
    stacked = jnp.stack([attn_key, attn_value])
    reach = (WINDOW - 2) // rows + 1
    earlier = []
    for back in range(reach, 0, -1):
        take = min(rows, WINDOW - 1 - (back - 1) * rows)
        got = from_behind(stacked[:, :, rows - take :], AA, back)
        moved = jnp.concatenate([jnp.zeros_like(got[:, :1]), got[:, :-1]], 1)
        earlier.append(jnp.where(index < back, moved, got))
    keys = jnp.concatenate(earlier + [stacked], 2)
    span = keys.shape[2]
    q = attn_query.reshape(stretches, rows, aheads, AD)
    k = keys[0].reshape(stretches, span, aheads, AD)
    v = keys[1].reshape(stretches, span, aheads, AD)
    scores = jnp.einsum("cqhe,ckhe->chqk", q, k, preferred_element_type=jnp.float32) / math.sqrt(AD)
    query_at = lax.broadcasted_iota(jnp.int32, (rows, span), 0)
    key_at = lax.broadcasted_iota(jnp.int32, (rows, span), 1)
    inside = (key_at >= query_at) & (key_at <= query_at + WINDOW - 1)
    stretch_at = jnp.arange(stretches, dtype=jnp.int32)[:, None]
    placed = (
        stretch_at * (rows * groups)
        + index * rows
        + jnp.arange(span, dtype=jnp.int32)[None, :]
        - (WINDOW - 1)
    )
    mask = inside[None, None] & (placed >= 0)[:, None, None, :]
    scores = jnp.where(mask, scores, -1e30)
    top = jnp.max(scores, -1, keepdims=True)
    probs = jnp.exp(scores - top)
    denom = jnp.sum(probs, -1)
    summed = jnp.einsum(
        "chqk,ckhe->cqhe", probs.astype(jnp.bfloat16), v, preferred_element_type=jnp.float32
    )
    attention = (summed / jnp.transpose(denom, (0, 2, 1))[..., None]).reshape(
        stretches, rows, aheads * AD
    )
    combined = (jnp.stack(fast_out) + attention).astype(jnp.bfloat16)
    arrived = exchange_by_chip(combined, ("ba_0", "ba_1"), (1, 0), 1, 2)
    values = arrived.astype(jnp.float32)
    scale = lax.rsqrt(jnp.mean(values * values, -1, keepdims=True) + EPS)
    mixed = (values * scale * gain).astype(jnp.bfloat16)
    return (mixed, weights, moment)


def solution(mesh):
    torus = Mesh(mesh.devices.reshape(4, 2, 4, 2, 2), ("aa_0", "aa_1", "aa_2", "ba_0", "ba_1"))
    return jax.shard_map(
        local,
        mesh=torus,
        in_specs=(
            P(None, AA, BA),
            P(None, AA, BA),
            P(None, AA, BA),
            P(None, AA, BA),
            P(None, AA, BA),
            P(None, AA, BA),
            P(None, AA, BA),
            P(AA, None, BA, None),
            P(),
        ),
        out_specs=(P(None, AA_BA, None), P(AA, None, BA, None), P(AA, None, BA, None)),
        check_vma=False,
    )
```

profile of v0, /device:TPU:0, one launch (start us, length us, event | category | flops | bytes accessed | tf_op | source)
XLA Modules:
  0.0 766.9 jit_solution(11554920662054973670)
XLA Ops:
  12.4 87.4 %all-gather.2.cloned.1.call-done = bf16[640,3,2,640]{3,2,1,0:T(2,128)(2,1)} async-done(((bf16[20,3,2,640]{3,2,1,0:T(2,128)(2,1)}), bf16[640,3,2,640]{3,2,1,0:T(2,128)(2,1)}) %all-gather.2.cloned.1.call-update) | async-done | bytes 4915216 | tf_op jit(solution)/shard_map/all_gather | solution.py:134
  118.0 358.9 %all-reduce.4.cloned.1.call-done = bf16[640,3,2,640]{3,0,2,1:T(8,128)(2,1)} async-done(((bf16[640,3,2,640]{3,0,2,1:T(8,128)(2,1)}), bf16[640,3,2,640]{3,0,2,1:T(8,128)(2,1)}) %all-reduce.4.cloned.1.call-update) | async-done | bytes 4915216 | tf_op jit(solution)/shard_map/psum | solution.py:142
  476.9 6.3 fusion.3
  483.2 9.2 %fusion.84 = (bf16[640,3,2,640]{3,0,2,1:T(8,128)(2,1)}, f32[640,3,2,640]{3,0,2,1:T(8,128)}) fusion(f32[3,2,640]{2,1,0:T(2,128)S(1)} %rsqrt_multiply_fusion.1, bf16[640,3,2,640]{3,0,2,1:T(8,128)(2,1)S(1)} %copy-done, bf16[640,3,2,640]{3,2,1,0:T(2,128)(2,1)} %all-gather.2.cloned.1.call-done), kind=kLoop, calls=%fused_computation.137 | loop fusion | flops 12288000 | bytes 24591360 | tf_op jit(solution)/shard_map/convert_element_type | solution.py:146
  507.0 8.4 %maximum_bitcast_fusion = bf16[4,4,2,20,3,2,640]{6,5,3,1,2,0,4:T(2,128)(2,1)S(1)} fusion(bf16[4,2,4,20,1,2,640]{6,5,3,2,1,0,4:T(2,128)(2,1)S(1)} %bitcast.208, bf16[4,2,4,20,1,2,640]{6,5,3,2,1,0,4:T(2,128)(2,1)S(1)} %bitcast.209, bf16[4,2,4,20,1,2,640]{6,5,3,2,1,0,4:T(2,128)(2,1)S(1)} %bitcast.210), kind=kLoop, calls=%fused_computation.17 | loop fusion | flops 4915200 | bytes 9830400 | tf_op jit(solution)/shard_map/transpose | solution.py:23
  515.3 3.7 copy.320
  522.7 7.6 copy.297
  543.8 52.4 %collective-permute-done = bf16[2,2,255,1280]{3,1,2,0:T(2,128)(2,1)} collective-permute-done((bf16[2,2,255,1280]{3,1,2,0:T(2,128)(2,1)}, bf16[2,2,255,1280]{3,1,2,0:T(2,128)(2,1)}, u32[]{:S(2)}, u32[]{:S(2)}) %collective-permute-start) | collective-permute-done | bytes 2611232 | tf_op jit(solution)/shard_map/ppermute | solution.py:50
  596.2 7.5 copy.298
  605.4 25.2 %collective-permute-done.1 = bf16[2,2,256,1280]{2,3,1,0:T(8,128)(2,1)} collective-permute-done((bf16[2,2,256,1280]{2,3,1,0:T(8,128)(2,1)}, bf16[2,2,256,1280]{2,3,1,0:T(8,128)(2,1)}, u32[]{:S(2)}, u32[]{:S(2)}) %collective-permute-start.1) | collective-permute-done | bytes 2621472 | tf_op jit(solution)/shard_map/ppermute | solution.py:50
  632.3 5.6 maximum_maximum_fusion
  639.2 7.3 fusion.2
  646.5 8.8 %fusion = f32[2,10,256]{2,1,0:T(8,128)S(1)} fusion(f32[2,10,767,256]{3,2,1,0:T(8,128)} %get-tuple-element.47, f32[2,10,256]{2,1,0:T(8,128)S(1)} %get-tuple-element.46, pred[2,256,767]{1,2,0:T(8,128)(4,1)S(1)} %broadcast_and_fusion), kind=kLoop, calls=%fused_computation.2 | loop fusion | flops 15703040 | bytes 16141824 | tf_op jit(solution)/shard_map/reduce_sum | solution.py:183
  655.3 11.0 %bitcast_divide_fusion = f32[2,256,10,128]{1,3,2,0:T(8,128)} fusion(bf16[2,767,10,128]{1,3,2,0:T(8,128)(2,1)S(1)} %bitcast.213, f32[2,10,767,256]{3,2,1,0:T(8,128)} %get-tuple-element.47, f32[2,10,256]{2,1,0:T(8,128)S(1)} %get-tuple-element.46, pred[2,256,767]{1,2,0:T(8,128)(4,1)S(1)} %broadcast_and_fusion, f32[2,256,10]{1,2,0:T(8,128)S(1)} %bitcast.230), kind=kOutput, calls=%fused_computation.24 | convolution fusion | flops 1021685760 | bytes 22690304 | tf_op jit(solution)/shard_map/chqk,ckhe->cqhe/dot_general | solution.py:184
  666.3 5.0 copy.304
  677.7 4.8 fusion.41
  685.9 3.5 stack.44
  692.5 4.8 fusion.38
  705.8 4.8 all_to_all.15
  711.7 3.6 all-to-all-start.1
  715.4 6.8 convert_element_type.79
  722.3 14.0 %all-to-all-done.1 = bf16[2,2,2,64,1280]{4,3,1,2,0:T(8,128)(2,1)S(1)} async-done(((bf16[2,2,2,64,1280]{4,3,1,2,0:T(8,128)(2,1)}), bf16[2,2,2,64,1280]{4,3,1,2,0:T(8,128)(2,1)S(1)}, u32[]{:S(2)}, u32[]{:S(2)}) %all-to-all-start.1) | async-done | bytes 1310752 | tf_op jit(solution)/shard_map/all_to_all | solution.py:63
  741.2 3.9 all-to-all-start.2
  747.4 10.3 %all-to-all-done.2 = f32[32,3,2,640]{3,2,1,0:T(2,128)S(1)} async-done(((f32[32,3,2,640]{3,2,1,0:T(2,128)}), f32[32,3,2,640]{3,2,1,0:T(2,128)S(1)}, u32[]{:S(2)}, u32[]{:S(2)}) %all-to-all-start.2) | async-done | bytes 491552 | tf_op jit(solution)/shard_map/all_to_all | solution.py:41
  (115 shorter events, 91.3 us)
Async XLA Ops:
  7.2 92.6 %all-gather.2.cloned.1.call-start = ((), (), s32[]{:S(2)}) async-start(), calls=%async_computation.6 | async-start | bytes 5068800 | tf_op jit(solution)/shard_map/all_gather | solution.py:134
  9.0 2.6 copy-start.5
  9.0 467.9 %all-reduce.4.cloned.1.call-start = ((), (), s32[]{:S(2)}) async-start(), calls=%async_computation.7 | async-start | bytes 9830400 | tf_op jit(solution)/shard_map/psum | solution.py:142
  11.6 0.7 copy-start.12
  102.8 2.2 copy-start.4
  103.5 1.6 copy-start.10
  111.2 566.4 %reduce-scatter.4.cloned.1.call-start = ((), (), s32[]{:S(2)}) async-start(), calls=%async_computation.8 | async-start | bytes 7372800 | tf_op jit(solution)/shard_map/reduce_scatter | solution.py:25
  476.9 6.3 copy-start
  492.5 2.3 copy-start.8
  494.8 2.2 copy-start.9
  519.0 1.3 copy-start.1
  519.0 203.2 %reduce-scatter.6.cloned.1.call-start = ((), (), s32[]{:S(2)}) async-start(), calls=%async_computation.9 | async-start | bytes 1843200 | tf_op jit(solution)/shard_map/reduce_scatter | solution.py:25
  530.3 65.9 %collective-permute-start = (bf16[2,2,255,1280]{3,1,2,0:T(2,128)(2,1)}, bf16[2,2,255,1280]{3,1,2,0:T(2,128)(2,1)}, u32[]{:S(2)}, u32[]{:S(2)}) collective-permute-start(bf16[2,2,255,1280]{3,1,2,0:T(2,128)(2,1)} %copy.297), channel_id=1, source_target_pairs={{0,8},{4,12},{8,16},{12,20},{16,24},{20,28},{24,32},{28,36},{32,40... | collective-permute-start | bytes 7833608 | tf_op jit(solution)/shard_map/ppermute | solution.py:50
  532.1 98.5 %collective-permute-start.1 = (bf16[2,2,256,1280]{2,3,1,0:T(8,128)(2,1)}, bf16[2,2,256,1280]{2,3,1,0:T(8,128)(2,1)}, u32[]{:S(2)}, u32[]{:S(2)}) collective-permute-start(bf16[2,2,256,1280]{2,3,1,0:T(8,128)(2,1)} %pad_maximum_fusion.1), channel_id=1, source_target_pairs={{0,4},{4,8},{8,12},{12,16},{16,20},{20,24},{24,28},{28,32},{32,36}... | collective-permute-start | bytes 7864328 | tf_op jit(solution)/shard_map/ppermute | solution.py:50
  603.8 1.3 slice-start
  637.9 1.3 copy-start.3
  671.3 3.1 copy-start.7
  685.9 3.5 copy-start.6
  711.7 24.6 %all-to-all-start.1 = ((bf16[2,2,2,64,1280]{4,3,1,2,0:T(8,128)(2,1)}), bf16[2,2,2,64,1280]{4,3,1,2,0:T(8,128)(2,1)S(1)}, u32[]{:S(2)}, u32[]{:S(2)}) async-start(bf16[2,2,2,64,1280]{4,3,1,2,0:T(8,128)(2,1)} %copy.306), calls=%async_computation.1 | async-start | bytes 2621440 | tf_op jit(solution)/shard_map/all_to_all | solution.py:63
  715.4 23.3 %reduce-scatter.8.cloned.1.call-start = ((), (), s32[]{:S(2)}) async-start(), calls=%async_computation.10 | async-start | bytes 552960 | tf_op jit(solution)/shard_map/reduce_scatter | solution.py:25
  738.6 6.5 copy-start.2
  738.6 6.5 copy-start.11
  741.2 16.6 %all-to-all-start.2 = ((f32[32,3,2,640]{3,2,1,0:T(2,128)}), f32[32,3,2,640]{3,2,1,0:T(2,128)S(1)}, u32[]{:S(2)}, u32[]{:S(2)}) async-start(f32[32,3,2,640]{3,2,1,0:T(2,128)} %broadcast_in_dim.12), calls=%async_computation.5 | async-start | bytes 983040 | tf_op jit(solution)/shard_map/all_to_all | solution.py:41
Sparse Core Ops, SparseCore 0:
  11.6 88.1 all-gather.1
  111.3 365.4 all-reduce.3
  519.2 61.7 reduce-scatter.3
  677.8 22.9 reduce-scatter.5
  722.4 15.5 reduce-scatter.7
where the time goes:
time: 774 us; the launch traced here: 767 us
  waiting for transfers between devices  548 us (71%)
  local copies, waits for them, and re-layouts  79.6 us (10%)
  other arithmetic  61.7 us (8%)
  matrix products  48.1 us (6%)
  between operations  14.6 us (2%)
  starting transfers between devices  9.74 us (1%)
    psum x1, waiting for transfers between devices, local(): lax.psum(term(0, full.shape[0]).astype(jnp.bfloat16), AA)  359 us
    all_gather x1, waiting for transfers between devices, local(): lax.all_gather(fast_weights.astype(jnp.bfloat16), AA, axis=0, tiled=True)  87.4 us
    ppermute x2, waiting for transfers between devices, from_behind(): lax.ppermute(shard, axis, [(i, (i + by) % length) for i in range(length)])  77.6 us
    unnamed x41, local copies, waits for them, and re-layouts  19.8 us
  transfers between devices with their start and end apart: 9, of which 6 were waited for; matrix products, arithmetic and copies ran while one was open for 16% of the time, Pallas kernels for 0%

commit v1 on v0

v1 whole, which is shorter than its diff:
```python
import math

import jax
import jax.numpy as jnp
from jax import lax
from jax.experimental import pallas as pl
from jax.experimental.pallas import tpu as pltpu
from jax.sharding import Mesh
from jax.sharding import PartitionSpec as P

AD = 128
WINDOW = 512
AA = ("aa_0", "aa_1", "aa_2")
BA = ("ba_0", "ba_1")
AA_BA = ("aa_0", "aa_1", "aa_2", "ba_0", "ba_1")
PLANE = ("aa_0", "aa_2")
PAIR = "aa_1"

BETA = 0.9
EPS = 1e-06


def activation(x):
    sig = jax.nn.sigmoid(x)
    return (x * sig, sig * (1.0 + x * (1.0 - sig)))


def partner(x):
    return lax.ppermute(x, PAIR, [(0, 1), (1, 0)])


def sent_to_all(shard, axis):
    copies = jnp.broadcast_to(shard, (lax.axis_size(axis), *shard.shape))
    return lax.all_to_all(copies, axis, split_axis=0, concat_axis=0, tiled=True)


def from_behind(shard, axis, by):
    length = lax.axis_size(axis)
    return lax.ppermute(shard, axis, [(i, (i + by) % length) for i in range(length)])


def times_t(x, w):
    return lax.dot_general(x, w, (((1,), (1,)), ((), ())), preferred_element_type=jnp.float32)


def t_times(x, y):
    return lax.dot_general(x, y, (((0,), (0,)), ((), ())), preferred_element_type=jnp.float32)


def matrices(full):
    depth = full.shape[-1]
    return [full[:, i].reshape(-1, depth) for i in range(3)]


def answers(gate, up, down, q):
    act, _ = activation(times_t(q, gate))
    hidden = (act * times_t(q, up)).astype(jnp.bfloat16)
    return jnp.dot(hidden, down, preferred_element_type=jnp.float32)


def gradient(gate, up, down, k, v, rate, parts):
    gate_in = times_t(k, gate)
    up_in = times_t(k, up)
    back_in = times_t(v, down)
    act, slope = activation(gate_in)
    gate_x = (rate[:, 0:1] * (-back_in * up_in * slope)).astype(jnp.bfloat16)
    up_x = (rate[:, 1:2] * (-back_in * act)).astype(jnp.bfloat16)
    down_x = (rate[:, 2:3] * -(act * up_in)).astype(jnp.bfloat16)
    terms = [t_times(gate_x, k), t_times(up_x, k), t_times(down_x, v)]
    return jnp.stack(
        [t.astype(jnp.bfloat16).reshape(parts, -1, t.shape[-1]) for t in terms], 1
    )


def summed_rows(terms):
    got = lax.all_to_all(terms, PLANE, split_axis=0, concat_axis=0, tiled=True)
    return jnp.sum(got.astype(jnp.float32), 0)


def attend_kernel(early_ref, q_ref, k0_ref, k1_ref, k2_ref, v0_ref, v1_ref, v2_ref, out_ref):
    c = pl.program_id(0)
    q = q_ref[0]
    rows = q.shape[0]
    scale = 1.0 / math.sqrt(AD)
    far = -1e30
    at_q = lax.broadcasted_iota(jnp.int32, (rows, rows), 0)
    at_k = lax.broadcasted_iota(jnp.int32, (rows, rows), 1)
    s0 = jnp.where(at_k <= at_q, times_t(q, k0_ref[0]) * scale, far)
    s1 = jnp.where(c >= early_ref[0], times_t(q, k1_ref[0]) * scale, far)
    s2 = jnp.where((at_k > at_q) & (c >= early_ref[1]), times_t(q, k2_ref[0]) * scale, far)
    top = jnp.max(jnp.maximum(jnp.maximum(s0, s1), s2), -1, keepdims=True)
    p0 = jnp.exp(s0 - top)
    p1 = jnp.exp(s1 - top)
    p2 = jnp.exp(s2 - top)
    denom = jnp.sum(p0 + p1 + p2, -1, keepdims=True)
    total = jnp.dot(p0.astype(jnp.bfloat16), v0_ref[0], preferred_element_type=jnp.float32)
    total += jnp.dot(p1.astype(jnp.bfloat16), v1_ref[0], preferred_element_type=jnp.float32)
    total += jnp.dot(p2.astype(jnp.bfloat16), v2_ref[0], preferred_element_type=jnp.float32)
    out_ref[0] = (total / denom).astype(out_ref.dtype)


def attend(early, q, keys, values):
    stretches, rows, width = q.shape
    block = (1, rows, AD)

    def own(c, h, early):
        return (c, 0, h)

    def behind(back):
        return lambda c, h, early: (jnp.maximum(c - early[back - 1], 0), 0, h)

    maps = [own, behind(1), behind(2)]
    specs = [pl.BlockSpec(block, m) for m in maps]
    return pl.pallas_call(
        attend_kernel,
        grid_spec=pltpu.PrefetchScalarGridSpec(
            num_scalar_prefetch=1,
            grid=(stretches, width // AD),
            in_specs=[pl.BlockSpec(block, own)] + specs + specs,
            out_specs=pl.BlockSpec(block, own),
        ),
        out_shape=jax.ShapeDtypeStruct(q.shape, jnp.bfloat16),
    )(early, q, *keys, *values)


def local(
    fast_query, fast_key, fast_value, rates, attn_query, attn_key, attn_value, fast_weights, gain
):
    stretches, rows, _ = fast_query.shape
    depth = fast_weights.shape[3]
    index = lax.axis_index(AA)
    first = lax.axis_index(PAIR) == 0
    parts = lax.axis_size(PLANE)

    def mine_and_other(a, b):
        return jnp.where(first, a, b), jnp.where(first, b, a)

    held = jnp.transpose(fast_weights.astype(jnp.bfloat16), (2, 1, 0, 3))
    mine, other = mine_and_other(held[0], held[1])
    chunk = jnp.concatenate([mine, partner(other)], 1)
    full = sent_to_all(chunk, PLANE)

    def swapped(x, c, size):
        a, b = mine_and_other(x[c, :, :size], x[c, :, size:])
        return jnp.concatenate([a, partner(b)], 0)

    keys = [swapped(fast_key, c, depth) for c in range(stretches)]
    values = [swapped(fast_value, c, depth) for c in range(stretches)]
    rate = [swapped(rates, c, 3) for c in range(stretches)]
    queries = [swapped(fast_query, c, depth) for c in range(stretches)]

    k1, v1 = from_behind(attn_key, AA, 1), from_behind(attn_value, AA, 1)
    k2, v2 = from_behind(attn_key, AA, 2), from_behind(attn_value, AA, 2)
    early = jnp.stack([index < 1, index < 2]).astype(jnp.int32)
    attention = attend(early, attn_query, (attn_key, k1, k2), (attn_value, v1, v2))

    def finish(out, c):
        back = partner(out[rows:].astype(jnp.bfloat16)).astype(jnp.float32)
        a, b = mine_and_other(out[:rows], back)
        combined = (jnp.concatenate([a, b], 1) + attention[c].astype(jnp.float32)).astype(
            jnp.bfloat16
        )
        size = lax.axis_size(BA)
        pieces = combined.reshape(size, rows // size, -1)
        got = lax.all_to_all(pieces, BA, split_axis=0, concat_axis=0, tiled=True)
        got = jnp.transpose(got, (1, 0, 2)).reshape(rows // size, -1).astype(jnp.float32)
        scale = lax.rsqrt(jnp.mean(got * got, -1, keepdims=True) + EPS)
        return (got * scale * gain).astype(jnp.bfloat16)

    wide = full.astype(jnp.float32)
    target = jnp.sqrt(jnp.sum(wide * wide, (0, 2)) + EPS)
    old = matrices(full)
    grads = summed_rows(gradient(*old, keys[0], values[0], rate[0], parts))
    out0 = answers(*old, queries[0])

    trial = wide - sent_to_all(grads.astype(jnp.bfloat16), PLANE).astype(jnp.float32)
    factor = target / jnp.sqrt(jnp.sum(trial * trial, (0, 2)) + EPS)
    new = matrices((trial * factor[None, :, None]).astype(jnp.bfloat16))
    own = (chunk.astype(jnp.float32) - grads) * factor[:, None]
    behind = grads * BETA
    local_rows = fast_weights.shape[0]
    own_other = partner(own[:, local_rows:])
    target_other = partner(target)

    moment = behind + summed_rows(gradient(*new, keys[1], values[1], rate[1], parts))
    out1 = answers(*new, queries[1])
    moment_other = partner(moment[:, local_rows:])
    last = own - moment
    squares = sent_to_all(jnp.sum(last * last, 1), AA)
    sides = [lax.axis_size(a) for a in AA]
    squares = jnp.sum(squares.reshape(*sides, 3, depth), (0, 2))
    squares, squares_other = mine_and_other(squares[0], squares[1])
    weights = last[:, :local_rows] * (target / jnp.sqrt(squares + EPS))[:, None]
    weights_other = (own_other - moment_other) * (
        target_other / jnp.sqrt(squares_other + EPS)
    )[:, None]

    def placed(a, b):
        return jnp.transpose(jnp.stack(mine_and_other(a, b)), (2, 1, 0, 3))

    mixed = jnp.stack([finish(out0, 0), finish(out1, 1)])
    return (
        mixed,
        placed(weights, weights_other),
        placed(moment[:, :local_rows], moment_other),
    )


def solution(mesh):
    torus = Mesh(mesh.devices.reshape(4, 2, 4, 2, 2), ("aa_0", "aa_1", "aa_2", "ba_0", "ba_1"))
    return jax.shard_map(
        local,
        mesh=torus,
        in_specs=(
            P(None, AA, BA),
            P(None, AA, BA),
            P(None, AA, BA),
            P(None, AA, BA),
            P(None, AA, BA),
            P(None, AA, BA),
            P(None, AA, BA),
            P(AA, None, BA, None),
            P(),
        ),
        out_specs=(P(None, AA_BA, None), P(AA, None, BA, None), P(AA, None, BA, None)),
        check_vma=False,
    )
```

time: 774 us -> 395 us (0.51)
  waiting for transfers between devices: 548 us -> 210 us
  starting transfers between devices: 9.74 us -> 71.8 us
  local copies, waits for them, and re-layouts: 79.6 us -> 25 us
  other arithmetic: 61.7 us -> 28.5 us
  Pallas kernels: 0 us -> 19.1 us
  between operations: 14.6 us -> 1.17 us
  matrix products: 48.1 us -> 36.8 us
    psum x1 -> x0, waiting for transfers between devices: 359 us -> none  [local(): lax.psum(term(0, full.shape[0]).astype(jnp.bfloat16), AA)]
    ppermute x0 -> x14, waiting for transfers between devices: none -> 122 us  [partner(): return lax.ppermute(x, PAIR, [(0, 1), (1, 0)])]
    all_gather x1 -> x0, waiting for transfers between devices: 87.4 us -> none  [local(): lax.all_gather(fast_weights.astype(jnp.bfloat16), AA, axis=0, tiled=True)]
    ppermute x2 -> x4, waiting for transfers between devices: 77.6 us -> 0.01 us  [from_behind(): lax.ppermute(shard, axis, [(i, (i + by) % length) for i in range(length)])]
    all_to_all x1 -> x3, waiting for transfers between devices: 10.3 us -> 47.1 us  [sent_to_all(): return lax.all_to_all(copies, axis, split_axis=0, concat_axis=0, tiled=True)]
    ppermute x0 -> x14, starting transfers between devices: none -> 28.4 us  [partner(): return lax.ppermute(x, PAIR, [(0, 1), (1, 0)])]
    all_to_all x1 -> x4, waiting for transfers between devices: 14 us -> 41.2 us  [the longest x2 28 us: summed_rows(): got = lax.all_to_all(terms, PLANE, split_axis=0, concat_axis=0, tiled=True)]
    pallas_call x0 -> x1, Pallas kernels: none -> 19.1 us  [attend(): pl.pallas_call(attend_kernel, grid_spec=pltpu.PrefetchScalarGridSpec(num_...]
  transfers between devices with their start and end apart: 9 -> 25, of which waited for: 6 -> 11; matrix products, arithmetic and copies ran while one was open for 16% -> 20% of each run, Pallas kernels for 0% -> 5%
where the time goes in v1:
time: 395 us; the launch traced here: 393 us
  waiting for transfers between devices  210 us (53%)
  starting transfers between devices  71.8 us (18%)
  matrix products  36.8 us (9%)
  other arithmetic  28.5 us (7%)
  local copies, waits for them, and re-layouts  25 us (6%)
  Pallas kernels  19.1 us (5%)
    ppermute x14, waiting for transfers between devices, partner(): return lax.ppermute(x, PAIR, [(0, 1), (1, 0)])  122 us
    all_to_all x3, waiting for transfers between devices, sent_to_all(): return lax.all_to_all(copies, axis, split_axis=0, concat_axis=0, tiled=True)  47.1 us
    ppermute x14, starting transfers between devices, partner(): return lax.ppermute(x, PAIR, [(0, 1), (1, 0)])  28.4 us
    all_to_all x2, waiting for transfers between devices, summed_rows(): got = lax.all_to_all(terms, PLANE, split_axis=0, concat_axis=0, tiled=True)  28 us
    pallas_call x1, Pallas kernels, attend(): pl.pallas_call(attend_kernel, grid_spec=pltpu.PrefetchScalarGridSpec(num_...  19.1 us
    all_to_all x3, starting transfers between devices, sent_to_all(): return lax.all_to_all(copies, axis, split_axis=0, concat_axis=0, tiled=True)  17.7 us
    dot_general x8, matrix products, times_t(): lax.dot_general(x, w, (((1,), (1,)), ((), ())), preferred_element_type=jn...  15.7 us
    all_to_all x2, waiting for transfers between devices, finish(): got = lax.all_to_all(pieces, BA, split_axis=0, concat_axis=0, tiled=True)  13.2 us
  transfers between devices with their start and end apart: 25, of which 11 were waited for; matrix products, arithmetic and copies ran while one was open for 20% of the time, Pallas kernels for 5%

profile of v1, /device:TPU:0, one launch (start us, length us, event | category | flops | bytes accessed | tf_op | source)
XLA Modules:
  0.0 392.5 jit_solution(11295538516617794306)
XLA Ops:
  2.1 4.1 %collective-permute-start.1 = (bf16[3,20,640]{2,1,0:T(8,128)(2,1)S(1)}, bf16[3,20,640]{2,1,0:T(8,128)(2,1)S(1)}, u32[]{:S(2)}, u32[]{:S(2)}) collective-permute-start(bf16[3,20,640]{2,1,0:T(8,128)(2,1)S(1)} %bitcast.140), channel_id=1, source_target_pairs={{0,16},{16,0},{1,17},{17,1},{2,18},{18,2},{3,19},{19,3},{4,20},{20... | collective-permute-start | bytes 230408 | tf_op jit(solution)/shard_map/ppermute | solution.py:29
  10.5 7.2 %all-to-all-start = ((bf16[16,3,40,640]{3,2,1,0:T(8,128)(2,1)}), bf16[16,3,40,640]{3,2,1,0:T(8,128)(2,1)S(1)}, u32[]{:S(2)}, u32[]{:S(2)}) async-start(bf16[16,3,40,640]{3,2,1,0:T(8,128)(2,1)} %broadcast_in_dim.6), calls=%async_computation | async-start | bytes 4915200 | tf_op jit(solution)/shard_map/all_to_all | solution.py:34
  24.7 3.4 collective-permute-start.6
  37.0 18.2 %all-to-all-done = bf16[16,3,40,640]{3,2,1,0:T(8,128)(2,1)S(1)} async-done(((bf16[16,3,40,640]{3,2,1,0:T(8,128)(2,1)}), bf16[16,3,40,640]{3,2,1,0:T(8,128)(2,1)S(1)}, u32[]{:S(2)}, u32[]{:S(2)}) %all-to-all-start) | async-done | bytes 2457632 | tf_op jit(solution)/shard_map/all_to_all | solution.py:34
  62.1 110.5 %collective-permute-done.9 = bf16[256,640]{1,0:T(8,128)(2,1)S(1)} collective-permute-done((bf16[256,640]{1,0:T(8,128)(2,1)S(1)}, bf16[256,640]{1,0:T(8,128)(2,1)S(1)}, u32[]{:S(2)}, u32[]{:S(2)}) %collective-permute-start.9) | collective-permute-done | bytes 327712 | tf_op jit(solution)/shard_map/ppermute | solution.py:29
  180.1 4.6 %all-to-all-start.2 = ((bf16[16,3,40,640]{3,2,1,0:T(8,128)(2,1)}), bf16[16,3,40,640]{3,2,1,0:T(8,128)(2,1)}, u32[]{:S(2)}, u32[]{:S(2)}) async-start(bf16[16,3,40,640]{3,2,1,0:T(8,128)(2,1)} %pad_maximum_fusion), calls=%async_computation.2 | async-start | bytes 4915200 | tf_op jit(solution)/shard_map/all_to_all | solution.py:76
  185.5 19.1 %shard_map.112 = bf16[2,256,1280]{2,1,0:T(8,128)(2,1)} custom-call(s32[2]{0:T(128)} %add_convert_fusion.early_ref, bf16[2,256,1280]{2,1,0:T(8,128)(2,1)} %q_ref.1, bf16[2,256,1280]{2,1,0:T(8,128)(2,1)} %k0_ref.1, bf16[2,256,1280]{2,1,0:T(8,128)(2,1)} %collective-permute-done.3.k1_ref, bf16[2,256,1280]{2,1,0:T(8,128)(2,1)} %collective-permute-done.4.k2_ref, ...), custom_call_target="tpu_custom_call" | custom-call | tf_op jit(solution)/shard_map/pallas_call | solution.py:114
  207.5 4.5 %fusion.11 = f32[512,640]{1,0:T(8,128)} fusion(bf16[640,640]{1,0:T(8,128)(2,1)} %bitcast.131, f32[512,640]{1,0:T(8,128)} %fusion.15, bf16[640,640]{1,0:T(8,128)(2,1)} %bitcast.118, bf16[256,640]{1,0:T(8,128)(2,1)} %collective-permute-done, bf16[256,640]{1,0:T(8,128)(2,1)} %get-tuple-element.56), kind=kOutput, calls=%fused_computation.58 | convolution fusion | flops 842137600 | bytes 4915200 | tf_op jit(solution)/shard_map/dot_general | solution.py:58
  213.1 3.5 collective-permute-start.2
  218.8 5.2 %collective-permute-done.2 = bf16[256,640]{1,0:T(8,128)(2,1)S(1)} collective-permute-done((bf16[256,640]{1,0:T(8,128)(2,1)S(1)}, bf16[256,640]{1,0:T(8,128)(2,1)S(1)}, u32[]{:S(2)}, u32[]{:S(2)}) %collective-permute-start.2) | collective-permute-done | bytes 327712 | tf_op jit(solution)/shard_map/ppermute | solution.py:29
  225.1 3.5 all-to-all-start.1
  231.4 7.4 %all-to-all-done.1 = bf16[4,64,1280]{2,1,0:T(8,128)(2,1)S(1)} async-done(((bf16[4,64,1280]{2,1,0:T(8,128)(2,1)}), bf16[4,64,1280]{2,1,0:T(8,128)(2,1)S(1)}, u32[]{:S(2)}, u32[]{:S(2)}) %all-to-all-start.1) | async-done | bytes 655392 | tf_op jit(solution)/shard_map/all_to_all | solution.py:165
  241.4 6.7 %all-to-all-start.3 = ((bf16[16,3,40,640]{3,2,1,0:T(8,128)(2,1)}), bf16[16,3,40,640]{3,2,1,0:T(8,128)(2,1)}, u32[]{:S(2)}, u32[]{:S(2)}) async-start(bf16[16,3,40,640]{3,2,1,0:T(8,128)(2,1)} %broadcast_in_dim.7), calls=%async_computation.3 | async-start | bytes 4915200 | tf_op jit(solution)/shard_map/all_to_all | solution.py:34
  248.1 3.1 collective-permute-start.12
  261.6 22.9 %all-to-all-done.3 = bf16[16,3,40,640]{3,2,1,0:T(8,128)(2,1)} async-done(((bf16[16,3,40,640]{3,2,1,0:T(8,128)(2,1)}), bf16[16,3,40,640]{3,2,1,0:T(8,128)(2,1)}, u32[]{:S(2)}, u32[]{:S(2)}) %all-to-all-start.3) | async-done | bytes 2457632 | tf_op jit(solution)/shard_map/all_to_all | solution.py:34
  293.6 4.0 %fusion.12 = f32[512,640]{1,0:T(8,128)} fusion(bf16[640,640]{1,0:T(8,128)(2,1)S(1)} %bitcast.134, f32[512,640]{1,0:T(8,128)} %fusion.13, bf16[640,640]{1,0:T(8,128)(2,1)S(1)} %bitcast.119, bf16[256,640]{1,0:T(8,128)(2,1)} %collective-permute-done.7, bf16[256,640]{1,0:T(8,128)(2,1)S(1)} %copy-done.8), kind=kOutput, calls=%fused_computation.59 | convolution fusion | flops 842137600 | bytes 4915200 | tf_op jit(solution)/shard_map/dot_general | solution.py:58
  298.7 3.4 collective-permute-start.11
  315.0 3.5 all-to-all-start.4
  322.9 5.8 %all-to-all-done.4 = bf16[4,64,1280]{2,1,0:T(8,128)(2,1)S(1)} async-done(((bf16[4,64,1280]{2,1,0:T(8,128)(2,1)}), bf16[4,64,1280]{2,1,0:T(8,128)(2,1)S(1)}, u32[]{:S(2)}, u32[]{:S(2)}) %all-to-all-start.4) | async-done | bytes 655392 | tf_op jit(solution)/shard_map/all_to_all | solution.py:165
  328.7 3.7 all-to-all-start.5
  341.8 28.0 %all-to-all-done.5 = bf16[16,3,40,640]{3,2,1,0:T(8,128)(2,1)S(1)} async-done(((bf16[16,3,40,640]{3,2,1,0:T(8,128)(2,1)}), bf16[16,3,40,640]{3,2,1,0:T(8,128)(2,1)S(1)}, u32[]{:S(2)}, u32[]{:S(2)}) %all-to-all-start.5) | async-done | bytes 2457632 | tf_op jit(solution)/shard_map/all_to_all | solution.py:76
  371.6 3.9 all-to-all-start.6
  376.6 3.3 collective-permute-start.15
  380.4 6.1 %all-to-all-done.6 = f32[32,3,640]{2,1,0:T(4,128)S(1)} async-done(((f32[32,3,640]{2,1,0:T(4,128)}), f32[32,3,640]{2,1,0:T(4,128)S(1)}, u32[]{:S(2)}, u32[]{:S(2)}) %all-to-all-start.6) | async-done | bytes 245792 | tf_op jit(solution)/shard_map/all_to_all | solution.py:34
  (142 shorter events, 105.9 us)
Async XLA Ops:
  2.1 6.7 %collective-permute-start.1 = (bf16[3,20,640]{2,1,0:T(8,128)(2,1)S(1)}, bf16[3,20,640]{2,1,0:T(8,128)(2,1)S(1)}, u32[]{:S(2)}, u32[]{:S(2)}) collective-permute-start(bf16[3,20,640]{2,1,0:T(8,128)(2,1)S(1)} %bitcast.140), channel_id=1, source_target_pairs={{0,16},{16,0},{1,17},{17,1},{2,18},{18,2},{3,19},{19,3},{4,20},{20... | collective-permute-start | bytes 230408 | tf_op jit(solution)/shard_map/ppermute | solution.py:29
  10.5 44.7 %all-to-all-start = ((bf16[16,3,40,640]{3,2,1,0:T(8,128)(2,1)}), bf16[16,3,40,640]{3,2,1,0:T(8,128)(2,1)S(1)}, u32[]{:S(2)}, u32[]{:S(2)}) async-start(bf16[16,3,40,640]{3,2,1,0:T(8,128)(2,1)} %broadcast_in_dim.6), calls=%async_computation | async-start | bytes 4915200 | tf_op jit(solution)/shard_map/all_to_all | solution.py:34
  17.7 167.8 %collective-permute-start.3 = (bf16[2,256,1280]{2,1,0:T(8,128)(2,1)}, bf16[2,256,1280]{2,1,0:T(8,128)(2,1)}, u32[]{:S(2)}, u32[]{:S(2)}) collective-permute-start(bf16[2,256,1280]{2,1,0:T(8,128)(2,1)} %k0_ref.1), channel_id=1, source_target_pairs={{0,4},{4,8},{8,12},{12,16},{16,20},{20,24},{24,28},{28,32},{32,36}... | collective-permute-start | bytes 3932168 | tf_op jit(solution)/shard_map/ppermute | solution.py:39
  19.6 165.8 %collective-permute-start.4 = (bf16[2,256,1280]{2,1,0:T(8,128)(2,1)}, bf16[2,256,1280]{2,1,0:T(8,128)(2,1)}, u32[]{:S(2)}, u32[]{:S(2)}) collective-permute-start(bf16[2,256,1280]{2,1,0:T(8,128)(2,1)} %k0_ref.1), channel_id=1, source_target_pairs={{0,8},{4,12},{8,16},{12,20},{16,24},{20,28},{24,32},{28,36},{32,40... | collective-permute-start | bytes 3932168 | tf_op jit(solution)/shard_map/ppermute | solution.py:39
  22.3 163.2 %collective-permute-start.5 = (bf16[2,256,1280]{2,1,0:T(8,128)(2,1)}, bf16[2,256,1280]{2,1,0:T(8,128)(2,1)}, u32[]{:S(2)}, u32[]{:S(2)}) collective-permute-start(bf16[2,256,1280]{2,1,0:T(8,128)(2,1)} %v0_ref.1), channel_id=1, source_target_pairs={{0,4},{4,8},{8,12},{12,16},{16,20},{20,24},{24,28},{28,32},{32,36}... | collective-permute-start | bytes 3932168 | tf_op jit(solution)/shard_map/ppermute | solution.py:39
  24.7 160.8 %collective-permute-start.6 = (bf16[2,256,1280]{2,1,0:T(8,128)(2,1)}, bf16[2,256,1280]{2,1,0:T(8,128)(2,1)}, u32[]{:S(2)}, u32[]{:S(2)}) collective-permute-start(bf16[2,256,1280]{2,1,0:T(8,128)(2,1)} %v0_ref.1), channel_id=1, source_target_pairs={{0,8},{4,12},{8,16},{12,20},{16,24},{20,28},{24,32},{28,36},{32,40... | collective-permute-start | bytes 3932168 | tf_op jit(solution)/shard_map/ppermute | solution.py:39
  34.5 20.9 %collective-permute-start.10 = (bf16[256,640]{1,0:T(8,128)(2,1)}, bf16[256,640]{1,0:T(8,128)(2,1)}, u32[]{:S(2)}, u32[]{:S(2)}) collective-permute-start(bf16[256,640]{1,0:T(8,128)(2,1)} %get-tuple-element.52), channel_id=1, source_target_pairs={{0,16},{16,0},{1,17},{17,1},{2,18},{18,2},{3,19},{19,3},{4,20},{20... | collective-permute-start | bytes 983048 | tf_op jit(solution)/shard_map/ppermute | solution.py:29
  56.2 116.4 %collective-permute-start.9 = (bf16[256,640]{1,0:T(8,128)(2,1)S(1)}, bf16[256,640]{1,0:T(8,128)(2,1)S(1)}, u32[]{:S(2)}, u32[]{:S(2)}) collective-permute-start(bf16[256,640]{1,0:T(8,128)(2,1)S(1)} %copy-done.17), channel_id=1, source_target_pairs={{0,16},{16,0},{1,17},{17,1},{2,18},{18,2},{3,19},{19,3},{4,20},{20... | collective-permute-start | bytes 983048 | tf_op jit(solution)/shard_map/ppermute | solution.py:29
  172.6 32.0 %collective-permute-start = (bf16[256,640]{1,0:T(8,128)(2,1)}, bf16[256,640]{1,0:T(8,128)(2,1)}, u32[]{:S(2)}, u32[]{:S(2)}) collective-permute-start(bf16[256,640]{1,0:T(8,128)(2,1)} %get-tuple-element.57), channel_id=1, source_target_pairs={{0,16},{16,0},{1,17},{17,1},{2,18},{18,2},{3,19},{19,3},{4,20},{20... | collective-permute-start | bytes 983048 | tf_op jit(solution)/shard_map/ppermute | solution.py:29
  180.1 45.0 %all-to-all-start.2 = ((bf16[16,3,40,640]{3,2,1,0:T(8,128)(2,1)}), bf16[16,3,40,640]{3,2,1,0:T(8,128)(2,1)}, u32[]{:S(2)}, u32[]{:S(2)}) async-start(bf16[16,3,40,640]{3,2,1,0:T(8,128)(2,1)} %pad_maximum_fusion), calls=%async_computation.2 | async-start | bytes 4915200 | tf_op jit(solution)/shard_map/all_to_all | solution.py:76
  213.1 10.9 %collective-permute-start.2 = (bf16[256,640]{1,0:T(8,128)(2,1)S(1)}, bf16[256,640]{1,0:T(8,128)(2,1)S(1)}, u32[]{:S(2)}, u32[]{:S(2)}) collective-permute-start(bf16[256,640]{1,0:T(8,128)(2,1)S(1)} %slice.236), channel_id=1, source_target_pairs={{0,16},{16,0},{1,17},{17,1},{2,18},{18,2},{3,19},{19,3},{4,20},{20... | collective-permute-start | bytes 983048 | tf_op jit(solution)/shard_map/ppermute | solution.py:29
  225.1 13.7 %all-to-all-start.1 = ((bf16[4,64,1280]{2,1,0:T(8,128)(2,1)}), bf16[4,64,1280]{2,1,0:T(8,128)(2,1)S(1)}, u32[]{:S(2)}, u32[]{:S(2)}) async-start(bf16[4,64,1280]{2,1,0:T(8,128)(2,1)} %fusion.3), calls=%async_computation.1 | async-start | bytes 1310720 | tf_op jit(solution)/shard_map/all_to_all | solution.py:165
  241.4 43.1 %all-to-all-start.3 = ((bf16[16,3,40,640]{3,2,1,0:T(8,128)(2,1)}), bf16[16,3,40,640]{3,2,1,0:T(8,128)(2,1)}, u32[]{:S(2)}, u32[]{:S(2)}) async-start(bf16[16,3,40,640]{3,2,1,0:T(8,128)(2,1)} %broadcast_in_dim.7), calls=%async_computation.3 | async-start | bytes 4915200 | tf_op jit(solution)/shard_map/all_to_all | solution.py:34
  248.1 7.1 %collective-permute-start.12 = (f32[256,3]{0,1:T(4,128)S(1)}, f32[256,3]{0,1:T(4,128)S(1)}, u32[]{:S(2)}, u32[]{:S(2)}) collective-permute-start(f32[256,3]{0,1:T(4,128)S(1)} %get-tuple-element.85), channel_id=1, source_target_pairs={{0,16},{16,0},{1,17},{17,1},{2,18},{18,2},{3,19},{19,3},{4,20},{20... | collective-permute-start | bytes 9224 | tf_op jit(solution)/shard_map/ppermute | solution.py:29
  251.2 54.7 %collective-permute-start.13 = (bf16[256,640]{1,0:T(8,128)(2,1)}, bf16[256,640]{1,0:T(8,128)(2,1)}, u32[]{:S(2)}, u32[]{:S(2)}) collective-permute-start(bf16[256,640]{1,0:T(8,128)(2,1)} %get-tuple-element.49), channel_id=1, source_target_pairs={{0,16},{16,0},{1,17},{17,1},{2,18},{18,2},{3,19},{19,3},{4,20},{20... | collective-permute-start | bytes 983048 | tf_op jit(solution)/shard_map/ppermute | solution.py:29
  251.7 50.4 %collective-permute-start.14 = (bf16[256,640]{1,0:T(8,128)(2,1)}, bf16[256,640]{1,0:T(8,128)(2,1)}, u32[]{:S(2)}, u32[]{:S(2)}) collective-permute-start(bf16[256,640]{1,0:T(8,128)(2,1)} %get-tuple-element.53), channel_id=1, source_target_pairs={{0,16},{16,0},{1,17},{17,1},{2,18},{18,2},{3,19},{19,3},{4,20},{20... | collective-permute-start | bytes 983048 | tf_op jit(solution)/shard_map/ppermute | solution.py:29
  254.8 35.3 %collective-permute-start.7 = (bf16[256,640]{1,0:T(8,128)(2,1)}, bf16[256,640]{1,0:T(8,128)(2,1)}, u32[]{:S(2)}, u32[]{:S(2)}) collective-permute-start(bf16[256,640]{1,0:T(8,128)(2,1)} %get-tuple-element.59), channel_id=1, source_target_pairs={{0,16},{16,0},{1,17},{17,1},{2,18},{18,2},{3,19},{19,3},{4,20},{20... | collective-permute-start | bytes 983048 | tf_op jit(solution)/shard_map/ppermute | solution.py:29
  298.7 14.2 %collective-permute-start.11 = (bf16[256,640]{1,0:T(8,128)(2,1)S(1)}, bf16[256,640]{1,0:T(8,128)(2,1)S(1)}, u32[]{:S(2)}, u32[]{:S(2)}) collective-permute-start(bf16[256,640]{1,0:T(8,128)(2,1)S(1)} %slice.235), channel_id=1, source_target_pairs={{0,16},{16,0},{1,17},{17,1},{2,18},{18,2},{3,19},{19,3},{4,20},{20... | collective-permute-start | bytes 983048 | tf_op jit(solution)/shard_map/ppermute | solution.py:29
  315.0 13.7 %all-to-all-start.4 = ((bf16[4,64,1280]{2,1,0:T(8,128)(2,1)}), bf16[4,64,1280]{2,1,0:T(8,128)(2,1)S(1)}, u32[]{:S(2)}, u32[]{:S(2)}) async-start(bf16[4,64,1280]{2,1,0:T(8,128)(2,1)} %fusion.4), calls=%async_computation.4 | async-start | bytes 1310720 | tf_op jit(solution)/shard_map/all_to_all | solution.py:165
  328.7 41.1 %all-to-all-start.5 = ((bf16[16,3,40,640]{3,2,1,0:T(8,128)(2,1)}), bf16[16,3,40,640]{3,2,1,0:T(8,128)(2,1)S(1)}, u32[]{:S(2)}, u32[]{:S(2)}) async-start(bf16[16,3,40,640]{3,2,1,0:T(8,128)(2,1)} %pad_maximum_fusion.1), calls=%async_computation.5 | async-start | bytes 4915200 | tf_op jit(solution)/shard_map/all_to_all | solution.py:76
  333.1 53.4 %collective-permute-start.17 = (f32[3,640]{1,0:T(4,128)S(1)}, f32[3,640]{1,0:T(4,128)}, u32[]{:S(2)}, u32[]{:S(2)}) collective-permute-start(f32[3,640]{1,0:T(4,128)S(1)} %get-tuple-element.76), channel_id=1, source_target_pairs={{0,16},{16,0},{1,17},{17,1},{2,18},{18,2},{3,19},{19,3},{4,20},{20... | collective-permute-start | bytes 23048 | tf_op jit(solution)/shard_map/ppermute | solution.py:29
  371.6 14.9 %all-to-all-start.6 = ((f32[32,3,640]{2,1,0:T(4,128)}), f32[32,3,640]{2,1,0:T(4,128)S(1)}, u32[]{:S(2)}, u32[]{:S(2)}) async-start(f32[32,3,640]{2,1,0:T(4,128)} %broadcast_in_dim.8), calls=%async_computation.6 | async-start | bytes 655360 | tf_op jit(solution)/shard_map/all_to_all | solution.py:34
  376.6 11.5 %collective-permute-start.15 = (f32[3,20,640]{2,1,0:T(8,128)S(1)}, f32[3,20,640]{2,1,0:T(8,128)S(1)}, u32[]{:S(2)}, u32[]{:S(2)}) collective-permute-start(f32[3,20,640]{2,1,0:T(8,128)S(1)} %slice.187), channel_id=1, source_target_pairs={{0,16},{16,0},{1,17},{17,1},{2,18},{18,2},{3,19},{19,3},{4,20},{20... | collective-permute-start | bytes 460808 | tf_op jit(solution)/shard_map/ppermute | solution.py:29
  379.9 10.7 %collective-permute-start.16 = (f32[3,20,640]{2,1,0:T(8,128)S(1)}, f32[3,20,640]{2,1,0:T(8,128)S(1)}, u32[]{:S(2)}, u32[]{:S(2)}) collective-permute-start(f32[3,20,640]{2,1,0:T(8,128)S(1)} %slice.188), channel_id=1, source_target_pairs={{0,16},{16,0},{1,17},{17,1},{2,18},{18,2},{3,19},{19,3},{4,20},{20... | collective-permute-start | bytes 460808 | tf_op jit(solution)/shard_map/ppermute | solution.py:29
  (23 other events, 317.1 us)

commit v2 on v1

--- a/solution.py
+++ b/solution.py
@@ -9,7 +9,6 @@
 from jax.sharding import PartitionSpec as P
 
 AD = 128
-WINDOW = 512
 AA = ("aa_0", "aa_1", "aa_2")
 BA = ("ba_0", "ba_1")
 AA_BA = ("aa_0", "aa_1", "aa_2", "ba_0", "ba_1")
@@ -32,6 +31,16 @@
 def sent_to_all(shard, axis):
     copies = jnp.broadcast_to(shard, (lax.axis_size(axis), *shard.shape))
     return lax.all_to_all(copies, axis, split_axis=0, concat_axis=0, tiled=True)
+
+
+def gathered(chunk):
+    row = sent_to_all(chunk, "aa_2")
+    return sent_to_all(row, "aa_0").reshape(-1, *chunk.shape)
+
+
+def after(x, done):
+    zero = jnp.minimum(jnp.abs(done.reshape(-1)[-1].astype(jnp.float32)), 0.0)
+    return x + zero.astype(x.dtype)
 
 
 def from_behind(shard, axis, by):
@@ -73,7 +82,11 @@
 
 
 def summed_rows(terms):
-    got = lax.all_to_all(terms, PLANE, split_axis=0, concat_axis=0, tiled=True)
+    side = lax.axis_size("aa_0")
+    terms = terms.reshape(side, -1, *terms.shape[1:])
+    got = lax.all_to_all(terms, "aa_0", split_axis=0, concat_axis=0, tiled=True)
+    rows = jnp.sum(got.astype(jnp.float32), 0).astype(jnp.bfloat16)
+    got = lax.all_to_all(rows, "aa_2", split_axis=0, concat_axis=0, tiled=True)
     return jnp.sum(got.astype(jnp.float32), 0)
 
 
@@ -123,7 +136,7 @@
     )(early, q, *keys, *values)
 
 
-def local(
+def step(
     fast_query, fast_key, fast_value, rates, attn_query, attn_key, attn_value, fast_weights, gain
 ):
     stretches, rows, _ = fast_query.shape
@@ -138,42 +151,41 @@
     held = jnp.transpose(fast_weights.astype(jnp.bfloat16), (2, 1, 0, 3))
     mine, other = mine_and_other(held[0], held[1])
     chunk = jnp.concatenate([mine, partner(other)], 1)
-    full = sent_to_all(chunk, PLANE)
+    full = gathered(chunk)
 
     def swapped(x, c, size):
         a, b = mine_and_other(x[c, :, :size], x[c, :, size:])
         return jnp.concatenate([a, partner(b)], 0)
 
-    keys = [swapped(fast_key, c, depth) for c in range(stretches)]
-    values = [swapped(fast_value, c, depth) for c in range(stretches)]
     rate = [swapped(rates, c, 3) for c in range(stretches)]
-    queries = [swapped(fast_query, c, depth) for c in range(stretches)]
-
-    k1, v1 = from_behind(attn_key, AA, 1), from_behind(attn_value, AA, 1)
-    k2, v2 = from_behind(attn_key, AA, 2), from_behind(attn_value, AA, 2)
-    early = jnp.stack([index < 1, index < 2]).astype(jnp.int32)
-    attention = attend(early, attn_query, (attn_key, k1, k2), (attn_value, v1, v2))
-
-    def finish(out, c):
-        back = partner(out[rows:].astype(jnp.bfloat16)).astype(jnp.float32)
-        a, b = mine_and_other(out[:rows], back)
-        combined = (jnp.concatenate([a, b], 1) + attention[c].astype(jnp.float32)).astype(
+    key0, value0 = swapped(fast_key, 0, depth), swapped(fast_value, 0, depth)
+    key1, value1 = swapped(fast_key, 1, depth), swapped(fast_value, 1, depth)
+    query0, query1 = swapped(fast_query, 0, depth), swapped(fast_query, 1, depth)
+    sent_key, sent_value = after(attn_key, key1), after(attn_value, value1)
+    k1, v1 = from_behind(sent_key, AA, 1), from_behind(sent_value, AA, 1)
+    k2, v2 = from_behind(sent_key, AA, 2), from_behind(sent_value, AA, 2)
+
+    def finish(outs, attention):
+        back = partner(jnp.stack([o[rows:] for o in outs]).astype(jnp.bfloat16))
+        a, b = mine_and_other(jnp.stack([o[:rows] for o in outs]), back.astype(jnp.float32))
+        combined = (jnp.concatenate([a, b], 2) + attention.astype(jnp.float32)).astype(
             jnp.bfloat16
         )
         size = lax.axis_size(BA)
-        pieces = combined.reshape(size, rows // size, -1)
+        pieces = jnp.moveaxis(combined.reshape(stretches, size, rows // size, -1), 1, 0)
         got = lax.all_to_all(pieces, BA, split_axis=0, concat_axis=0, tiled=True)
-        got = jnp.transpose(got, (1, 0, 2)).reshape(rows // size, -1).astype(jnp.float32)
+        got = jnp.transpose(got, (1, 2, 0, 3)).reshape(stretches, rows // size, -1)
+        got = got.astype(jnp.float32)
         scale = lax.rsqrt(jnp.mean(got * got, -1, keepdims=True) + EPS)
         return (got * scale * gain).astype(jnp.bfloat16)
 
     wide = full.astype(jnp.float32)
     target = jnp.sqrt(jnp.sum(wide * wide, (0, 2)) + EPS)
     old = matrices(full)
-    grads = summed_rows(gradient(*old, keys[0], values[0], rate[0], parts))
-    out0 = answers(*old, queries[0])
-
-    trial = wide - sent_to_all(grads.astype(jnp.bfloat16), PLANE).astype(jnp.float32)
+    terms = gradient(*old, key0, value0, rate[0], parts)
+    grads = summed_rows(terms)
+
+    trial = wide - gathered(grads.astype(jnp.bfloat16)).astype(jnp.float32)
     factor = target / jnp.sqrt(jnp.sum(trial * trial, (0, 2)) + EPS)
     new = matrices((trial * factor[None, :, None]).astype(jnp.bfloat16))
     own = (chunk.astype(jnp.float32) - grads) * factor[:, None]
@@ -182,8 +194,12 @@
     own_other = partner(own[:, local_rows:])
     target_other = partner(target)
 
-    moment = behind + summed_rows(gradient(*new, keys[1], values[1], rate[1], parts))
-    out1 = answers(*new, queries[1])
+    terms = gradient(*new, key1, value1, rate[1], parts)
+    moment = behind + summed_rows(terms)
+    out0 = answers(*old, after(query0, terms))
+    out1 = answers(*new, after(query1, terms))
+    early = after(jnp.stack([index < 1, index < 2]).astype(jnp.int32), terms)
+    attention = attend(early, attn_query, (attn_key, k1, k2), (attn_value, v1, v2))
     moment_other = partner(moment[:, local_rows:])
     last = own - moment
     squares = sent_to_all(jnp.sum(last * last, 1), AA)
@@ -198,7 +214,7 @@
     def placed(a, b):
         return jnp.transpose(jnp.stack(mine_and_other(a, b)), (2, 1, 0, 3))
 
-    mixed = jnp.stack([finish(out0, 0), finish(out1, 1)])
+    mixed = finish([out0, out1], attention)
     return (
         mixed,
         placed(weights, weights_other),
@@ -209,7 +225,7 @@
 def solution(mesh):
     torus = Mesh(mesh.devices.reshape(4, 2, 4, 2, 2), ("aa_0", "aa_1", "aa_2", "ba_0", "ba_1"))
     return jax.shard_map(
-        local,
+        step,
         mesh=torus,
         in_specs=(
             P(None, AA, BA),

time: 395 us -> 419 us (1.061)
  waiting for transfers between devices: 210 us -> 97.1 us
  starting transfers between devices: 71.8 us -> 136 us
  blocking collectives: 0 us -> 55.9 us
  local copies, waits for them, and re-layouts: 25 us -> 35.6 us
  other arithmetic: 28.5 us -> 38.3 us
  matrix products: 36.8 us -> 30 us
    ppermute x14 -> x13, waiting for transfers between devices: 122 us -> 51.7 us  [partner(): return lax.ppermute(x, PAIR, [(0, 1), (1, 0)])]
    ppermute x14 -> x13, starting transfers between devices: 28.4 us -> 95.4 us  [partner(): return lax.ppermute(x, PAIR, [(0, 1), (1, 0)])]
    all_to_all x0 -> x3, blocking collectives: none -> 55.9 us  [the longest x1 30.9 us: summed_rows(): got = lax.all_to_all(terms, 'aa_0', split_axis=0, concat_axis=0, tiled=True)]
    all_to_all x3 -> x4, waiting for transfers between devices: 47.1 us -> 24.8 us  [sent_to_all(): return lax.all_to_all(copies, axis, split_axis=0, concat_axis=0, tiled=True)]
    all_to_all x2, waiting for transfers between devices: 28 us -> 7.67 us  [the longest x1 7.66 us: summed_rows(): got = lax.all_to_all(rows, 'aa_2', split_axis=0, concat_axis=0, tiled=True)]
    reshape x0 -> x4, local copies, waits for them, and re-layouts: none -> 11 us  [the longest x3 9.82 us: after(): zero = jnp.minimum(jnp.abs(done.reshape(-1)[-1].astype(jnp.float32)), 0.0)]
    convert_element_type x4 -> x1, local copies, waits for them, and re-layouts: 9.66 us -> 1.77 us  [finish(): got = got.astype(jnp.float32)]
    reduce_sum x3 -> x5, other arithmetic: 3.03 us -> 9.12 us  [the longest x2 4.33 us: summed_rows(): rows = jnp.sum(got.astype(jnp.float32), 0).astype(jnp.bfloat16)]
  transfers between devices with their start and end apart: 25 -> 24, of which waited for: 11 -> 10; matrix products, arithmetic and copies ran while one was open for 20% -> 20% of each run, Pallas kernels for 5% -> 5%
where the time goes in v2:
time: 419 us; the launch traced here: 416 us
  starting transfers between devices  136 us (32%)
  waiting for transfers between devices  97.1 us (23%)
  blocking collectives  55.9 us (13%)
  other arithmetic  38.3 us (9%)
  local copies, waits for them, and re-layouts  35.6 us (8%)
  matrix products  30 us (7%)
  Pallas kernels  19.1 us (5%)
    ppermute x13, starting transfers between devices, partner(): return lax.ppermute(x, PAIR, [(0, 1), (1, 0)])  95.4 us
    ppermute x13, waiting for transfers between devices, partner(): return lax.ppermute(x, PAIR, [(0, 1), (1, 0)])  51.7 us
    all_to_all x1, blocking collectives, summed_rows(): got = lax.all_to_all(terms, 'aa_0', split_axis=0, concat_axis=0, tiled=True)  30.9 us
    all_to_all x4, waiting for transfers between devices, sent_to_all(): return lax.all_to_all(copies, axis, split_axis=0, concat_axis=0, tiled=True)  24.8 us
    all_to_all x4, starting transfers between devices, sent_to_all(): return lax.all_to_all(copies, axis, split_axis=0, concat_axis=0, tiled=True)  22 us
    pallas_call x1, Pallas kernels, attend(): pl.pallas_call(attend_kernel, grid_spec=pltpu.PrefetchScalarGridSpec(num_...  19.1 us
    all_to_all x1, blocking collectives, sent_to_all(): return lax.all_to_all(copies, axis, split_axis=0, concat_axis=0, tiled=True)  14 us
    dot_general x8, matrix products, times_t(): lax.dot_general(x, w, (((1,), (1,)), ((), ())), preferred_element_type=jn...  13.5 us
  transfers between devices with their start and end apart: 24, of which 10 were waited for; matrix products, arithmetic and copies ran while one was open for 20% of the time, Pallas kernels for 5%

profile of v2, /device:TPU:0, one launch (start us, length us, event | category | flops | bytes accessed | tf_op | source)
XLA Modules:
  0.0 415.5 jit_solution(2301520108168386856)
XLA Ops:
  2.1 4.1 collective-permute-start.3
  9.6 14.0 %all_to_all.50 = bf16[4,3,40,640]{3,2,1,0:T(8,128)(2,1)S(1)} all-to-all(bf16[4,3,40,640]{3,2,1,0:T(8,128)(2,1)S(1)} %broadcast_in_dim.10), channel_id=1, replica_groups=mesh['aa_0'=4,'aa_1'=2,'aa_2'=4,'ba_0'=2,'ba_1'=2] {'aa_2'}, dimensions={0} | all-to-all | bytes 1228800 | tf_op jit(solution)/shard_map/all_to_all | solution.py:33
  25.1 4.5 %all-to-all-start.1 = ((bf16[4,4,3,40,640]{4,3,2,1,0:T(8,128)(2,1)}), bf16[4,4,3,40,640]{4,3,2,1,0:T(8,128)(2,1)S(1)}, u32[]{:S(2)}, u32[]{:S(2)}) async-start(bf16[4,4,3,40,640]{4,3,2,1,0:T(8,128)(2,1)} %broadcast_in_dim.22), calls=%async_computation.1 | async-start | bytes 4915200 | tf_op jit(solution)/shard_map/all_to_all | solution.py:33
  39.6 4.6 %collective-permute-done.4 = f32[256,3]{0,1:T(4,128)S(1)} collective-permute-done((f32[256,3]{0,1:T(4,128)S(1)}, f32[256,3]{0,1:T(4,128)S(1)}, u32[]{:S(2)}, u32[]{:S(2)}) %collective-permute-start.4) | collective-permute-done | bytes 3104 | tf_op jit(solution)/shard_map/ppermute | solution.py:28
  44.1 14.0 %all-to-all-done.1 = bf16[4,4,3,40,640]{4,3,2,1,0:T(8,128)(2,1)S(1)} async-done(((bf16[4,4,3,40,640]{4,3,2,1,0:T(8,128)(2,1)}), bf16[4,4,3,40,640]{4,3,2,1,0:T(8,128)(2,1)S(1)}, u32[]{:S(2)}, u32[]{:S(2)}) %all-to-all-start.1) | async-done | bytes 2457632 | tf_op jit(solution)/shard_map/all_to_all | solution.py:33
  66.4 30.9 %all_to_all.51 = bf16[4,4,3,40,640]{4,3,1,2,0:T(8,128)(2,1)} all-to-all(bf16[4,4,3,40,640]{4,3,1,2,0:T(8,128)(2,1)S(1)} %pad_maximum_fusion), channel_id=1, replica_groups=mesh['aa_0'=4,'aa_1'=2,'aa_2'=4,'ba_0'=2,'ba_1'=2] {'aa_0'}, dimensions={0} | all-to-all | bytes 4915200 | tf_op jit(solution)/shard_map/all_to_all | solution.py:87
  99.6 11.0 %all_to_all.52 = bf16[4,3,40,640]{3,2,1,0:T(8,128)(2,1)S(1)} all-to-all(bf16[4,3,40,640]{3,2,1,0:T(8,128)(2,1)S(1)} %copy.235), channel_id=1, replica_groups=mesh['aa_0'=4,'aa_1'=2,'aa_2'=4,'ba_0'=2,'ba_1'=2] {'aa_2'}, dimensions={0} | all-to-all | bytes 1228800 | tf_op jit(solution)/shard_map/all_to_all | solution.py:89
  112.2 4.2 %all-to-all-start.4 = ((bf16[4,3,40,640]{3,2,1,0:T(8,128)(2,1)}), bf16[4,3,40,640]{3,2,1,0:T(8,128)(2,1)}, u32[]{:S(2)}, u32[]{:S(2)}) async-start(bf16[4,3,40,640]{3,2,1,0:T(8,128)(2,1)} %broadcast_in_dim.23), calls=%async_computation.4 | async-start | bytes 1228800 | tf_op jit(solution)/shard_map/all_to_all | solution.py:33
  120.0 5.0 %all-to-all-done.4 = bf16[4,3,40,640]{3,2,1,0:T(8,128)(2,1)} async-done(((bf16[4,3,40,640]{3,2,1,0:T(8,128)(2,1)}), bf16[4,3,40,640]{3,2,1,0:T(8,128)(2,1)}, u32[]{:S(2)}, u32[]{:S(2)}) %all-to-all-start.4) | async-done | bytes 614432 | tf_op jit(solution)/shard_map/all_to_all | solution.py:33
  127.8 4.5 %all-to-all-start.5 = ((bf16[4,4,3,40,640]{4,3,2,1,0:T(8,128)(2,1)}), bf16[4,4,3,40,640]{4,3,2,1,0:T(8,128)(2,1)}, u32[]{:S(2)}, u32[]{:S(2)}) async-start(bf16[4,4,3,40,640]{4,3,2,1,0:T(8,128)(2,1)} %broadcast_in_dim.24), calls=%async_computation.5 | async-start | bytes 4915200 | tf_op jit(solution)/shard_map/all_to_all | solution.py:33
  178.8 4.8 %all-to-all-start.7 = ((bf16[4,4,3,40,640]{4,3,1,2,0:T(8,128)(2,1)}), bf16[4,4,3,40,640]{4,3,1,2,0:T(8,128)(2,1)S(1)}, u32[]{:S(2)}, u32[]{:S(2)}) async-start(bf16[4,4,3,40,640]{4,3,1,2,0:T(8,128)(2,1)} %pad_maximum_fusion.2), calls=%async_computation.7 | async-start | bytes 4915200 | tf_op jit(solution)/shard_map/all_to_all | solution.py:87
  186.7 5.3 %reshape.151 = bf16[1228800]{0:T(1024)(128)(2,1)} reshape(bf16[16,3,40,640]{3,2,1,0:T(8,128)(2,1)} %pad_maximum_fusion.1) | data formatting | bytes 4915200 | tf_op jit(solution)/shard_map/reshape | solution.py:42
  198.1 4.3 %fusion.13 = f32[512,640]{1,0:T(8,128)} fusion(bf16[640,640]{1,0:T(8,128)(2,1)} %bitcast.161, f32[512,640]{1,0:T(8,128)} %fusion.17, bf16[640,640]{1,0:T(8,128)(2,1)S(1)} %bitcast.151, bf16[256,640]{1,0:T(8,128)(2,1)} %collective-permute-done, bf16[256,640]{1,0:T(8,128)(2,1)} %get-tuple-element.50, bf16[]{:T(256)} %bitcast.43), kind=kOutput, calls=%fused_computation.60 | convolution fusion | flops 842792960 | bytes 4915202 | tf_op jit(solution)/shard_map/dot_general | solution.py:67
  204.2 42.0 %collective-permute-done.8 = bf16[256,640]{1,0:T(8,128)(2,1)} collective-permute-done((bf16[256,640]{1,0:T(8,128)(2,1)}, bf16[256,640]{1,0:T(8,128)(2,1)}, u32[]{:S(2)}, u32[]{:S(2)}) %collective-permute-start.8) | collective-permute-done | bytes 327712 | tf_op jit(solution)/shard_map/ppermute | solution.py:28
  249.6 4.3 %fusion.14 = f32[512,640]{1,0:T(8,128)} fusion(bf16[640,640]{1,0:T(8,128)(2,1)} %bitcast.163, f32[512,640]{1,0:T(8,128)} %fusion.15, bf16[640,640]{1,0:T(8,128)(2,1)S(1)} %bitcast.155, bf16[256,640]{1,0:T(8,128)(2,1)} %collective-permute-done.8, bf16[256,640]{1,0:T(8,128)(2,1)} %get-tuple-element.52, bf16[]{:T(256)} %bitcast.43), kind=kOutput, calls=%fused_computation.61 | convolution fusion | flops 842792960 | bytes 4915202 | tf_op jit(solution)/shard_map/dot_general | solution.py:67
  256.8 71.1 %collective-permute-start.9 = (bf16[2,256,640]{2,1,0:T(8,128)(2,1)}, bf16[2,256,640]{2,1,0:T(8,128)(2,1)S(1)}, u32[]{:S(2)}, u32[]{:S(2)}) collective-permute-start(bf16[2,256,640]{2,1,0:T(8,128)(2,1)} %pad_maximum_fusion.8), channel_id=1, source_target_pairs={{0,16},{16,0},{1,17},{17,1},{2,18},{18,2},{3,19},{19,3},{4,20},{20... | collective-permute-start | bytes 1966088 | tf_op jit(solution)/shard_map/ppermute | solution.py:28
  328.6 19.1 %shard_map.112 = bf16[2,256,1280]{2,1,0:T(8,128)(2,1)} custom-call(s32[2]{0:T(128)} %fusion.35.early_ref, bf16[2,256,1280]{2,1,0:T(8,128)(2,1)} %q_ref.1, bf16[2,256,1280]{2,1,0:T(8,128)(2,1)} %k0_ref.1, bf16[2,256,1280]{2,1,0:T(8,128)(2,1)} %collective-permute-done.10.k1_ref, bf16[2,256,1280]{2,1,0:T(8,128)(2,1)} %collective-permute-done.11.k2_ref, ...), custom_call_target="tpu_custom_call" | custom-call | tf_op jit(solution)/shard_map/pallas_call | solution.py:127
  353.4 3.5 all-to-all-start.6
  361.3 13.0 %all-to-all-done.6 = bf16[4,2,64,1280]{3,2,1,0:T(8,128)(2,1)S(1)} async-done(((bf16[4,2,64,1280]{3,2,1,0:T(8,128)(2,1)}), bf16[4,2,64,1280]{3,2,1,0:T(8,128)(2,1)S(1)}, u32[]{:S(2)}, u32[]{:S(2)}) %all-to-all-start.6) | async-done | bytes 1310752 | tf_op jit(solution)/shard_map/all_to_all | solution.py:176
  374.2 4.2 %all-to-all-start.8 = ((bf16[4,3,40,640]{3,2,1,0:T(8,128)(2,1)}), bf16[4,3,40,640]{3,2,1,0:T(8,128)(2,1)S(1)}, u32[]{:S(2)}, u32[]{:S(2)}) async-start(bf16[4,3,40,640]{3,2,1,0:T(8,128)(2,1)} %copy.245), calls=%async_computation.8 | async-start | bytes 1228800 | tf_op jit(solution)/shard_map/all_to_all | solution.py:89
  380.8 7.7 %all-to-all-done.8 = bf16[4,3,40,640]{3,2,1,0:T(8,128)(2,1)S(1)} async-done(((bf16[4,3,40,640]{3,2,1,0:T(8,128)(2,1)}), bf16[4,3,40,640]{3,2,1,0:T(8,128)(2,1)S(1)}, u32[]{:S(2)}, u32[]{:S(2)}) %all-to-all-start.8) | async-done | bytes 614432 | tf_op jit(solution)/shard_map/all_to_all | solution.py:89
  390.3 8.8 %all-to-all-start.9 = ((f32[32,3,640]{2,1,0:T(4,128)}), f32[32,3,640]{2,1,0:T(4,128)}, u32[]{:S(2)}, u32[]{:S(2)}) async-start(f32[32,3,640]{2,1,0:T(4,128)} %broadcast_in_dim.25), calls=%async_computation.9 | async-start | bytes 655360 | tf_op jit(solution)/shard_map/all_to_all | solution.py:33
  400.6 3.3 collective-permute-start.14
  404.3 5.8 %all-to-all-done.9 = f32[32,3,640]{2,1,0:T(4,128)} async-done(((f32[32,3,640]{2,1,0:T(4,128)}), f32[32,3,640]{2,1,0:T(4,128)}, u32[]{:S(2)}, u32[]{:S(2)}) %all-to-all-start.9) | async-done | bytes 245792 | tf_op jit(solution)/shard_map/all_to_all | solution.py:33
  (174 shorter events, 118.5 us)
Async XLA Ops:
  2.1 6.7 %collective-permute-start.3 = (bf16[3,20,640]{2,1,0:T(8,128)(2,1)S(1)}, bf16[3,20,640]{2,1,0:T(8,128)(2,1)S(1)}, u32[]{:S(2)}, u32[]{:S(2)}) collective-permute-start(bf16[3,20,640]{2,1,0:T(8,128)(2,1)S(1)} %bitcast.167), channel_id=1, source_target_pairs={{0,16},{16,0},{1,17},{17,1},{2,18},{18,2},{3,19},{19,3},{4,20},{20... | collective-permute-start | bytes 230408 | tf_op jit(solution)/shard_map/ppermute | solution.py:28
  25.1 32.9 %all-to-all-start.1 = ((bf16[4,4,3,40,640]{4,3,2,1,0:T(8,128)(2,1)}), bf16[4,4,3,40,640]{4,3,2,1,0:T(8,128)(2,1)S(1)}, u32[]{:S(2)}, u32[]{:S(2)}) async-start(bf16[4,4,3,40,640]{4,3,2,1,0:T(8,128)(2,1)} %broadcast_in_dim.22), calls=%async_computation.1 | async-start | bytes 4915200 | tf_op jit(solution)/shard_map/all_to_all | solution.py:33
  32.0 26.4 %collective-permute-start.6 = (bf16[256,640]{1,0:T(8,128)(2,1)}, bf16[256,640]{1,0:T(8,128)(2,1)S(1)}, u32[]{:S(2)}, u32[]{:S(2)}) collective-permute-start(bf16[256,640]{1,0:T(8,128)(2,1)} %get-tuple-element.60), channel_id=1, source_target_pairs={{0,16},{16,0},{1,17},{17,1},{2,18},{18,2},{3,19},{19,3},{4,20},{20... | collective-permute-start | bytes 983048 | tf_op jit(solution)/shard_map/ppermute | solution.py:28
  34.8 9.3 %collective-permute-start.4 = (f32[256,3]{0,1:T(4,128)S(1)}, f32[256,3]{0,1:T(4,128)S(1)}, u32[]{:S(2)}, u32[]{:S(2)}) collective-permute-start(f32[256,3]{0,1:T(4,128)S(1)} %get-tuple-element.87), channel_id=1, source_target_pairs={{0,16},{16,0},{1,17},{17,1},{2,18},{18,2},{3,19},{19,3},{4,20},{20... | collective-permute-start | bytes 9224 | tf_op jit(solution)/shard_map/ppermute | solution.py:28
  36.7 23.6 %collective-permute-start.5 = (bf16[256,640]{1,0:T(8,128)(2,1)}, bf16[256,640]{1,0:T(8,128)(2,1)}, u32[]{:S(2)}, u32[]{:S(2)}) collective-permute-start(bf16[256,640]{1,0:T(8,128)(2,1)} %get-tuple-element.57), channel_id=1, source_target_pairs={{0,16},{16,0},{1,17},{17,1},{2,18},{18,2},{3,19},{19,3},{4,20},{20... | collective-permute-start | bytes 983048 | tf_op jit(solution)/shard_map/ppermute | solution.py:28
  112.2 12.8 %all-to-all-start.4 = ((bf16[4,3,40,640]{3,2,1,0:T(8,128)(2,1)}), bf16[4,3,40,640]{3,2,1,0:T(8,128)(2,1)}, u32[]{:S(2)}, u32[]{:S(2)}) async-start(bf16[4,3,40,640]{3,2,1,0:T(8,128)(2,1)} %broadcast_in_dim.23), calls=%async_computation.4 | async-start | bytes 1228800 | tf_op jit(solution)/shard_map/all_to_all | solution.py:33
  116.4 34.3 %collective-permute-start.2 = (bf16[256,640]{1,0:T(8,128)(2,1)}, bf16[256,640]{1,0:T(8,128)(2,1)}, u32[]{:S(2)}, u32[]{:S(2)}) collective-permute-start(bf16[256,640]{1,0:T(8,128)(2,1)} %get-tuple-element.55), channel_id=1, source_target_pairs={{0,16},{16,0},{1,17},{17,1},{2,18},{18,2},{3,19},{19,3},{4,20},{20... | collective-permute-start | bytes 983048 | tf_op jit(solution)/shard_map/ppermute | solution.py:28
  118.0 22.5 %collective-permute-start.7 = (bf16[256,640]{1,0:T(8,128)(2,1)S(1)}, bf16[256,640]{1,0:T(8,128)(2,1)S(1)}, u32[]{:S(2)}, u32[]{:S(2)}) collective-permute-start(bf16[256,640]{1,0:T(8,128)(2,1)S(1)} %copy-done.24), channel_id=1, source_target_pairs={{0,16},{16,0},{1,17},{17,1},{2,18},{18,2},{3,19},{19,3},{4,20},{20... | collective-permute-start | bytes 983048 | tf_op jit(solution)/shard_map/ppermute | solution.py:28
  127.8 34.4 %all-to-all-start.5 = ((bf16[4,4,3,40,640]{4,3,2,1,0:T(8,128)(2,1)}), bf16[4,4,3,40,640]{4,3,2,1,0:T(8,128)(2,1)}, u32[]{:S(2)}, u32[]{:S(2)}) async-start(bf16[4,4,3,40,640]{4,3,2,1,0:T(8,128)(2,1)} %broadcast_in_dim.24), calls=%async_computation.5 | async-start | bytes 4915200 | tf_op jit(solution)/shard_map/all_to_all | solution.py:33
  132.3 7.6 %collective-permute-start.1 = (f32[256,3]{0,1:T(4,128)S(1)}, f32[256,3]{0,1:T(4,128)S(1)}, u32[]{:S(2)}, u32[]{:S(2)}) collective-permute-start(f32[256,3]{0,1:T(4,128)S(1)} %get-tuple-element.85), channel_id=1, source_target_pairs={{0,16},{16,0},{1,17},{17,1},{2,18},{18,2},{3,19},{19,3},{4,20},{20... | collective-permute-start | bytes 9224 | tf_op jit(solution)/shard_map/ppermute | solution.py:28
  136.4 57.6 %collective-permute-start = (bf16[256,640]{1,0:T(8,128)(2,1)}, bf16[256,640]{1,0:T(8,128)(2,1)}, u32[]{:S(2)}, u32[]{:S(2)}) collective-permute-start(bf16[256,640]{1,0:T(8,128)(2,1)} %get-tuple-element.51), channel_id=1, source_target_pairs={{0,16},{16,0},{1,17},{17,1},{2,18},{18,2},{3,19},{19,3},{4,20},{20... | collective-permute-start | bytes 983048 | tf_op jit(solution)/shard_map/ppermute | solution.py:28
  138.4 107.9 %collective-permute-start.8 = (bf16[256,640]{1,0:T(8,128)(2,1)}, bf16[256,640]{1,0:T(8,128)(2,1)}, u32[]{:S(2)}, u32[]{:S(2)}) collective-permute-start(bf16[256,640]{1,0:T(8,128)(2,1)} %get-tuple-element.53), channel_id=1, source_target_pairs={{0,16},{16,0},{1,17},{17,1},{2,18},{18,2},{3,19},{19,3},{4,20},{20... | collective-permute-start | bytes 983048 | tf_op jit(solution)/shard_map/ppermute | solution.py:28
  148.1 180.5 %collective-permute-start.10 = (bf16[2,256,1280]{2,1,0:T(8,128)(2,1)}, bf16[2,256,1280]{2,1,0:T(8,128)(2,1)}, u32[]{:S(2)}, u32[]{:S(2)}) collective-permute-start(bf16[2,256,1280]{2,1,0:T(8,128)(2,1)} %broadcast_add_fusion.1), channel_id=1, source_target_pairs={{0,4},{4,8},{8,12},{12,16},{16,20},{20,24},{24,28},{28,32},{32,36}... | collective-permute-start | bytes 3932168 | tf_op jit(solution)/shard_map/ppermute | solution.py:48
  148.7 179.9 %collective-permute-start.11 = (bf16[2,256,1280]{2,1,0:T(8,128)(2,1)}, bf16[2,256,1280]{2,1,0:T(8,128)(2,1)}, u32[]{:S(2)}, u32[]{:S(2)}) collective-permute-start(bf16[2,256,1280]{2,1,0:T(8,128)(2,1)} %broadcast_add_fusion.1), channel_id=1, source_target_pairs={{0,8},{4,12},{8,16},{12,20},{16,24},{20,28},{24,32},{28,36},{32,40... | collective-permute-start | bytes 3932168 | tf_op jit(solution)/shard_map/ppermute | solution.py:48
  159.2 169.3 %collective-permute-start.12 = (bf16[2,256,1280]{2,1,0:T(8,128)(2,1)}, bf16[2,256,1280]{2,1,0:T(8,128)(2,1)}, u32[]{:S(2)}, u32[]{:S(2)}) collective-permute-start(bf16[2,256,1280]{2,1,0:T(8,128)(2,1)} %broadcast_add_fusion), channel_id=1, source_target_pairs={{0,4},{4,8},{8,12},{12,16},{16,20},{20,24},{24,28},{28,32},{32,36}... | collective-permute-start | bytes 3932168 | tf_op jit(solution)/shard_map/ppermute | solution.py:48
  178.8 173.2 %all-to-all-start.7 = ((bf16[4,4,3,40,640]{4,3,1,2,0:T(8,128)(2,1)}), bf16[4,4,3,40,640]{4,3,1,2,0:T(8,128)(2,1)S(1)}, u32[]{:S(2)}, u32[]{:S(2)}) async-start(bf16[4,4,3,40,640]{4,3,1,2,0:T(8,128)(2,1)} %pad_maximum_fusion.2), calls=%async_computation.7 | async-start | bytes 4915200 | tf_op jit(solution)/shard_map/all_to_all | solution.py:87
  194.0 134.6 %collective-permute-start.13 = (bf16[2,256,1280]{2,1,0:T(8,128)(2,1)}, bf16[2,256,1280]{2,1,0:T(8,128)(2,1)}, u32[]{:S(2)}, u32[]{:S(2)}) collective-permute-start(bf16[2,256,1280]{2,1,0:T(8,128)(2,1)} %broadcast_add_fusion), channel_id=1, source_target_pairs={{0,8},{4,12},{8,16},{12,20},{16,24},{20,28},{24,32},{28,36},{32,40... | collective-permute-start | bytes 3932168 | tf_op jit(solution)/shard_map/ppermute | solution.py:48
  256.8 92.4 %collective-permute-start.9 = (bf16[2,256,640]{2,1,0:T(8,128)(2,1)}, bf16[2,256,640]{2,1,0:T(8,128)(2,1)S(1)}, u32[]{:S(2)}, u32[]{:S(2)}) collective-permute-start(bf16[2,256,640]{2,1,0:T(8,128)(2,1)} %pad_maximum_fusion.8), channel_id=1, source_target_pairs={{0,16},{16,0},{1,17},{17,1},{2,18},{18,2},{3,19},{19,3},{4,20},{20... | collective-permute-start | bytes 1966088 | tf_op jit(solution)/shard_map/ppermute | solution.py:28
  353.4 20.9 %all-to-all-start.6 = ((bf16[4,2,64,1280]{3,2,1,0:T(8,128)(2,1)}), bf16[4,2,64,1280]{3,2,1,0:T(8,128)(2,1)S(1)}, u32[]{:S(2)}, u32[]{:S(2)}) async-start(bf16[4,2,64,1280]{3,2,1,0:T(8,128)(2,1)} %bitcast.143), calls=%async_computation.6 | async-start | bytes 2621440 | tf_op jit(solution)/shard_map/all_to_all | solution.py:176
  356.9 54.2 %collective-permute-start.16 = (f32[3,640]{1,0:T(4,128)S(1)}, f32[3,640]{1,0:T(4,128)S(1)}, u32[]{:S(2)}, u32[]{:S(2)}) collective-permute-start(f32[3,640]{1,0:T(4,128)S(1)} %copy-done.30), channel_id=1, source_target_pairs={{0,16},{16,0},{1,17},{17,1},{2,18},{18,2},{3,19},{19,3},{4,20},{20... | collective-permute-start | bytes 23048 | tf_op jit(solution)/shard_map/ppermute | solution.py:28
  374.2 14.3 %all-to-all-start.8 = ((bf16[4,3,40,640]{3,2,1,0:T(8,128)(2,1)}), bf16[4,3,40,640]{3,2,1,0:T(8,128)(2,1)S(1)}, u32[]{:S(2)}, u32[]{:S(2)}) async-start(bf16[4,3,40,640]{3,2,1,0:T(8,128)(2,1)} %copy.245), calls=%async_computation.8 | async-start | bytes 1228800 | tf_op jit(solution)/shard_map/all_to_all | solution.py:89
  390.3 19.8 %all-to-all-start.9 = ((f32[32,3,640]{2,1,0:T(4,128)}), f32[32,3,640]{2,1,0:T(4,128)}, u32[]{:S(2)}, u32[]{:S(2)}) async-start(f32[32,3,640]{2,1,0:T(4,128)} %broadcast_in_dim.25), calls=%async_computation.9 | async-start | bytes 655360 | tf_op jit(solution)/shard_map/all_to_all | solution.py:33
  400.6 10.8 %collective-permute-start.14 = (f32[3,20,640]{2,1,0:T(8,128)S(1)}, f32[3,20,640]{2,1,0:T(8,128)S(1)}, u32[]{:S(2)}, u32[]{:S(2)}) collective-permute-start(f32[3,20,640]{2,1,0:T(8,128)S(1)} %slice.194), channel_id=1, source_target_pairs={{0,16},{16,0},{1,17},{17,1},{2,18},{18,2},{3,19},{19,3},{4,20},{20... | collective-permute-start | bytes 460808 | tf_op jit(solution)/shard_map/ppermute | solution.py:28
  404.0 9.6 %collective-permute-start.15 = (f32[3,20,640]{2,1,0:T(8,128)S(1)}, f32[3,20,640]{2,1,0:T(8,128)S(1)}, u32[]{:S(2)}, u32[]{:S(2)}) collective-permute-start(f32[3,20,640]{2,1,0:T(8,128)S(1)} %slice.195), channel_id=1, source_target_pairs={{0,16},{16,0},{1,17},{17,1},{2,18},{18,2},{3,19},{19,3},{4,20},{20... | collective-permute-start | bytes 460808 | tf_op jit(solution)/shard_map/ppermute | solution.py:28
  (32 other events, 130.0 us)

commit v3 on v2

--- a/solution.py
+++ b/solution.py
@@ -33,9 +33,12 @@
     return lax.all_to_all(copies, axis, split_axis=0, concat_axis=0, tiled=True)
 
 
-def gathered(chunk):
-    row = sent_to_all(chunk, "aa_2")
-    return sent_to_all(row, "aa_0").reshape(-1, *chunk.shape)
+def gathered_row(chunk):
+    return sent_to_all(chunk, "aa_2")
+
+
+def gathered(row):
+    return sent_to_all(row, "aa_0").reshape(-1, *row.shape[1:])
 
 
 def after(x, done):
@@ -81,11 +84,13 @@
     )
 
 
-def summed_rows(terms):
+def summed_rows(terms, *done):
     side = lax.axis_size("aa_0")
     terms = terms.reshape(side, -1, *terms.shape[1:])
     got = lax.all_to_all(terms, "aa_0", split_axis=0, concat_axis=0, tiled=True)
     rows = jnp.sum(got.astype(jnp.float32), 0).astype(jnp.bfloat16)
+    for d in done:
+        rows = after(rows, d)
     got = lax.all_to_all(rows, "aa_2", split_axis=0, concat_axis=0, tiled=True)
     return jnp.sum(got.astype(jnp.float32), 0)
 
@@ -151,7 +156,7 @@
     held = jnp.transpose(fast_weights.astype(jnp.bfloat16), (2, 1, 0, 3))
     mine, other = mine_and_other(held[0], held[1])
     chunk = jnp.concatenate([mine, partner(other)], 1)
-    full = gathered(chunk)
+    full = gathered(gathered_row(chunk))
 
     def swapped(x, c, size):
         a, b = mine_and_other(x[c, :, :size], x[c, :, size:])
@@ -160,10 +165,8 @@
     rate = [swapped(rates, c, 3) for c in range(stretches)]
     key0, value0 = swapped(fast_key, 0, depth), swapped(fast_value, 0, depth)
     key1, value1 = swapped(fast_key, 1, depth), swapped(fast_value, 1, depth)
-    query0, query1 = swapped(fast_query, 0, depth), swapped(fast_query, 1, depth)
     sent_key, sent_value = after(attn_key, key1), after(attn_value, value1)
     k1, v1 = from_behind(sent_key, AA, 1), from_behind(sent_value, AA, 1)
-    k2, v2 = from_behind(sent_key, AA, 2), from_behind(sent_value, AA, 2)
 
     def finish(outs, attention):
         back = partner(jnp.stack([o[rows:] for o in outs]).astype(jnp.bfloat16))
@@ -183,9 +186,15 @@
     target = jnp.sqrt(jnp.sum(wide * wide, (0, 2)) + EPS)
     old = matrices(full)
     terms = gradient(*old, key0, value0, rate[0], parts)
-    grads = summed_rows(terms)
-
-    trial = wide - gathered(grads.astype(jnp.bfloat16)).astype(jnp.float32)
+    grads = summed_rows(terms, k1, v1)
+    row = gathered_row(grads.astype(jnp.bfloat16))
+    sent_key, sent_value = after(k1, row), after(v1, row)
+    k2, v2 = from_behind(sent_key, AA, 1), from_behind(sent_value, AA, 1)
+    change = gathered(row)
+    queries = after(fast_query, v1)
+    query0, query1 = swapped(queries, 0, depth), swapped(queries, 1, depth)
+
+    trial = wide - change.astype(jnp.float32)
     factor = target / jnp.sqrt(jnp.sum(trial * trial, (0, 2)) + EPS)
     new = matrices((trial * factor[None, :, None]).astype(jnp.bfloat16))
     own = (chunk.astype(jnp.float32) - grads) * factor[:, None]

time: 419 us -> 398 us (0.950)
  starting transfers between devices: 136 us -> 94.5 us
  blocking collectives: 55.9 us -> 26 us
  waiting for transfers between devices: 97.1 us -> 124 us
  local copies, waits for them, and re-layouts: 35.6 us -> 47.6 us
  other arithmetic: 38.3 us -> 44 us
    ppermute x13, starting transfers between devices: 95.4 us -> 60.3 us  [partner(): return lax.ppermute(x, PAIR, [(0, 1), (1, 0)])]
    all_to_all x1 -> x0, blocking collectives: 30.9 us -> none  [summed_rows(): got = lax.all_to_all(terms, 'aa_0', split_axis=0, concat_axis=0, tiled=True)]
    ppermute x4, waiting for transfers between devices: 0.01 us -> 24.3 us  [from_behind(): lax.ppermute(shard, axis, [(i, (i + by) % length) for i in range(length)])]
    reshape x3 -> x6, local copies, waits for them, and re-layouts: 9.82 us -> 18.7 us  [after(): zero = jnp.minimum(jnp.abs(done.reshape(-1)[-1].astype(jnp.float32)), 0.0)]
    add x3 -> x7, other arithmetic: 5.59 us -> 12 us  [after(): return x + zero.astype(x.dtype)]
    ppermute x4, starting transfers between devices: 6.41 us -> 0.57 us  [from_behind(): lax.ppermute(shard, axis, [(i, (i + by) % length) for i in range(length)])]
    all_to_all x1 -> x2, starting transfers between devices: 4.8 us -> 8.53 us  [summed_rows(): got = lax.all_to_all(terms, 'aa_0', split_axis=0, concat_axis=0, tiled=True)]
  transfers between devices with their start and end apart: 24 -> 25, of which waited for: 10 -> 13; matrix products, arithmetic and copies ran while one was open for 20% -> 28% of each run, Pallas kernels for 5% -> 5%
where the time goes in v3:
time: 398 us; the launch traced here: 394 us
  waiting for transfers between devices  124 us (31%)
  starting transfers between devices  94.5 us (24%)
  local copies, waits for them, and re-layouts  47.6 us (12%)
  other arithmetic  44 us (11%)
  matrix products  33.9 us (9%)
  blocking collectives  26 us (7%)
  Pallas kernels  19.1 us (5%)
  between operations  5.36 us (1%)
    ppermute x13, starting transfers between devices, partner(): return lax.ppermute(x, PAIR, [(0, 1), (1, 0)])  60.3 us
    ppermute x13, waiting for transfers between devices, partner(): return lax.ppermute(x, PAIR, [(0, 1), (1, 0)])  49.9 us
    all_to_all x4, waiting for transfers between devices, sent_to_all(): return lax.all_to_all(copies, axis, split_axis=0, concat_axis=0, tiled=True)  27.8 us
    ppermute x4, waiting for transfers between devices, from_behind(): lax.ppermute(shard, axis, [(i, (i + by) % length) for i in range(length)])  24.3 us
    pallas_call x1, Pallas kernels, attend(): pl.pallas_call(attend_kernel, grid_spec=pltpu.PrefetchScalarGridSpec(num_...  19.1 us
    reshape x6, local copies, waits for them, and re-layouts, after(): zero = jnp.minimum(jnp.abs(done.reshape(-1)[-1].astype(jnp.float32)), 0.0)  18.7 us
    all_to_all x4, starting transfers between devices, sent_to_all(): return lax.all_to_all(copies, axis, split_axis=0, concat_axis=0, tiled=True)  18.1 us
    dot_general x8, matrix products, times_t(): lax.dot_general(x, w, (((1,), (1,)), ((), ())), preferred_element_type=jn...  15.5 us
  transfers between devices with their start and end apart: 25, of which 13 were waited for; matrix products, arithmetic and copies ran while one was open for 28% of the time, Pallas kernels for 5%

profile of v3, /device:TPU:0, one launch (start us, length us, event | category | flops | bytes accessed | tf_op | source)
XLA Modules:
  0.0 394.4 jit_solution(7099001173642841755)
XLA Ops:
  2.1 4.1 %collective-permute-start.4 = (bf16[3,20,640]{2,1,0:T(8,128)(2,1)S(1)}, bf16[3,20,640]{2,1,0:T(8,128)(2,1)S(1)}, u32[]{:S(2)}, u32[]{:S(2)}) collective-permute-start(bf16[3,20,640]{2,1,0:T(8,128)(2,1)S(1)} %bitcast.172), channel_id=1, source_target_pairs={{0,16},{16,0},{1,17},{17,1},{2,18},{18,2},{3,19},{19,3},{4,20},{20... | collective-permute-start | bytes 230408 | tf_op jit(solution)/shard_map/ppermute | solution.py:28
  9.6 14.0 %all_to_all.50 = bf16[4,3,40,640]{3,2,1,0:T(8,128)(2,1)S(1)} all-to-all(bf16[4,3,40,640]{3,2,1,0:T(8,128)(2,1)S(1)} %broadcast_in_dim.10), channel_id=1, replica_groups=mesh['aa_0'=4,'aa_1'=2,'aa_2'=4,'ba_0'=2,'ba_1'=2] {'aa_2'}, dimensions={0} | all-to-all | bytes 1228800 | tf_op jit(solution)/shard_map/all_to_all | solution.py:33
  25.2 4.5 %all-to-all-start.1 = ((bf16[4,4,3,40,640]{4,3,2,1,0:T(8,128)(2,1)}), bf16[4,4,3,40,640]{4,3,2,1,0:T(8,128)(2,1)S(1)}, u32[]{:S(2)}, u32[]{:S(2)}) async-start(bf16[4,4,3,40,640]{4,3,2,1,0:T(8,128)(2,1)} %broadcast_in_dim.22), calls=%async_computation.1 | async-start | bytes 4915200 | tf_op jit(solution)/shard_map/all_to_all | solution.py:33
  44.4 7.0 %collective-permute-done.8 = bf16[256,640]{1,0:T(8,128)(2,1)S(1)} collective-permute-done((bf16[256,640]{1,0:T(8,128)(2,1)S(1)}, bf16[256,640]{1,0:T(8,128)(2,1)S(1)}, u32[]{:S(2)}, u32[]{:S(2)}) %collective-permute-start.8) | collective-permute-done | bytes 327712 | tf_op jit(solution)/shard_map/ppermute | solution.py:28
  59.6 30.9 %collective-permute-done = bf16[256,640]{1,0:T(8,128)(2,1)} collective-permute-done((bf16[256,640]{1,0:T(8,128)(2,1)}, bf16[256,640]{1,0:T(8,128)(2,1)}, u32[]{:S(2)}, u32[]{:S(2)}) %collective-permute-start) | collective-permute-done | bytes 327712 | tf_op jit(solution)/shard_map/ppermute | solution.py:28
  110.6 4.5 %all-to-all-start.2 = ((bf16[4,4,3,40,640]{4,3,1,2,0:T(8,128)(2,1)}), bf16[4,4,3,40,640]{4,3,1,2,0:T(8,128)(2,1)}, u32[]{:S(2)}, u32[]{:S(2)}) async-start(bf16[4,4,3,40,640]{4,3,1,2,0:T(8,128)(2,1)} %pad_maximum_fusion), calls=%async_computation.2 | async-start | bytes 4915200 | tf_op jit(solution)/shard_map/all_to_all | solution.py:90
  117.7 3.8 reshape.180
  123.4 24.3 %collective-permute-done.1.v1_ref = bf16[2,256,1280]{2,1,0:T(8,128)(2,1)} collective-permute-done((bf16[2,256,1280]{2,1,0:T(8,128)(2,1)}, bf16[2,256,1280]{2,1,0:T(8,128)(2,1)}, u32[]{:S(2)}, u32[]{:S(2)}) %collective-permute-start.1) | collective-permute-done | bytes 1310752 | tf_op jit(solution)/shard_map/ppermute | solution.py:51
  147.7 3.8 reshape.177
  155.8 12.0 %all_to_all.51 = bf16[4,3,40,640]{3,2,1,0:T(8,128)(2,1)S(1)} all-to-all(bf16[4,3,40,640]{3,2,1,0:T(8,128)(2,1)S(1)} %copy.235), channel_id=1, replica_groups=mesh['aa_0'=4,'aa_1'=2,'aa_2'=4,'ba_0'=2,'ba_1'=2] {'aa_2'}, dimensions={0} | all-to-all | bytes 1228800 | tf_op jit(solution)/shard_map/all_to_all | solution.py:94
  172.4 5.1 %collective-permute-done.3 = f32[256,3]{0,1:T(4,128)S(1)} collective-permute-done((f32[256,3]{0,1:T(4,128)S(1)}, f32[256,3]{0,1:T(4,128)S(1)}, u32[]{:S(2)}, u32[]{:S(2)}) %collective-permute-start.3) | collective-permute-done | bytes 3104 | tf_op jit(solution)/shard_map/ppermute | solution.py:28
  177.5 6.6 %all-to-all-done.4 = bf16[4,3,40,640]{3,2,1,0:T(8,128)(2,1)S(1)} async-done(((bf16[4,3,40,640]{3,2,1,0:T(8,128)(2,1)}), bf16[4,3,40,640]{3,2,1,0:T(8,128)(2,1)S(1)}, u32[]{:S(2)}, u32[]{:S(2)}) %all-to-all-start.4) | async-done | bytes 614432 | tf_op jit(solution)/shard_map/all_to_all | solution.py:33
  185.8 4.5 %all-to-all-start.5 = ((bf16[4,4,3,40,640]{4,3,2,1,0:T(8,128)(2,1)}), bf16[4,4,3,40,640]{4,3,2,1,0:T(8,128)(2,1)}, u32[]{:S(2)}, u32[]{:S(2)}) async-start(bf16[4,4,3,40,640]{4,3,2,1,0:T(8,128)(2,1)} %broadcast_in_dim.24), calls=%async_computation.5 | async-start | bytes 4915200 | tf_op jit(solution)/shard_map/all_to_all | solution.py:33
  204.7 15.4 %all-to-all-done.5 = bf16[4,4,3,40,640]{4,3,2,1,0:T(8,128)(2,1)} async-done(((bf16[4,4,3,40,640]{4,3,2,1,0:T(8,128)(2,1)}), bf16[4,4,3,40,640]{4,3,2,1,0:T(8,128)(2,1)}, u32[]{:S(2)}, u32[]{:S(2)}) %all-to-all-start.5) | async-done | bytes 2457632 | tf_op jit(solution)/shard_map/all_to_all | solution.py:33
  236.8 4.0 %all-to-all-start.7 = ((bf16[4,4,3,40,640]{4,3,1,2,0:T(8,128)(2,1)}), bf16[4,4,3,40,640]{4,3,1,2,0:T(8,128)(2,1)S(1)}, u32[]{:S(2)}, u32[]{:S(2)}) async-start(bf16[4,4,3,40,640]{4,3,1,2,0:T(8,128)(2,1)} %pad_maximum_fusion.2), calls=%async_computation.7 | async-start | bytes 4915200 | tf_op jit(solution)/shard_map/all_to_all | solution.py:90
  244.0 5.3 %reshape.181 = bf16[1228800]{0:T(1024)(128)(2,1)} reshape(bf16[16,3,40,640]{3,2,1,0:T(8,128)(2,1)} %pad_maximum_fusion.1) | data formatting | bytes 4915200 | tf_op jit(solution)/shard_map/reshape | solution.py:45
  254.5 4.3 %fusion.13 = f32[512,640]{1,0:T(8,128)} fusion(bf16[640,640]{1,0:T(8,128)(2,1)} %bitcast.166, f32[512,640]{1,0:T(8,128)} %fusion.17, bf16[640,640]{1,0:T(8,128)(2,1)S(1)} %bitcast.156, bf16[256,640]{1,0:T(8,128)(2,1)} %collective-permute-done.2, bf16[256,640]{1,0:T(8,128)(2,1)} %get-tuple-element.50, bf16[]{:T(256)} %bitcast.47), kind=kOutput, calls=%fused_computation.63 | convolution fusion | flops 842792960 | bytes 4915202 | tf_op jit(solution)/shard_map/dot_general | solution.py:70
  263.8 4.3 %fusion.14 = f32[512,640]{1,0:T(8,128)} fusion(bf16[640,640]{1,0:T(8,128)(2,1)} %bitcast.168, f32[512,640]{1,0:T(8,128)} %fusion.15, bf16[640,640]{1,0:T(8,128)(2,1)S(1)} %bitcast.160, bf16[256,640]{1,0:T(8,128)(2,1)} %collective-permute-done.10, bf16[256,640]{1,0:T(8,128)(2,1)} %get-tuple-element.52, bf16[]{:T(256)} %bitcast.47), kind=kOutput, calls=%fused_computation.64 | convolution fusion | flops 842792960 | bytes 4915202 | tf_op jit(solution)/shard_map/dot_general | solution.py:70
  271.1 38.9 %collective-permute-start.11 = (bf16[2,256,640]{2,1,0:T(8,128)(2,1)}, bf16[2,256,640]{2,1,0:T(8,128)(2,1)S(1)}, u32[]{:S(2)}, u32[]{:S(2)}) collective-permute-start(bf16[2,256,640]{2,1,0:T(8,128)(2,1)} %pad_maximum_fusion.8), channel_id=1, source_target_pairs={{0,16},{16,0},{1,17},{17,1},{2,18},{18,2},{3,19},{19,3},{4,20},{20... | collective-permute-start | bytes 1966088 | tf_op jit(solution)/shard_map/ppermute | solution.py:28
  310.6 19.1 %shard_map.112 = bf16[2,256,1280]{2,1,0:T(8,128)(2,1)} custom-call(s32[2]{0:T(128)} %fusion.35.early_ref, bf16[2,256,1280]{2,1,0:T(8,128)(2,1)} %q_ref.1, bf16[2,256,1280]{2,1,0:T(8,128)(2,1)} %k0_ref.1, bf16[2,256,1280]{2,1,0:T(8,128)(2,1)} %collective-permute-done.9.k1_ref, bf16[2,256,1280]{2,1,0:T(8,128)(2,1)} %collective-permute-done.12.k2_ref, ...), custom_call_target="tpu_custom_call" | custom-call | tf_op jit(solution)/shard_map/pallas_call | solution.py:132
  342.1 14.2 %all-to-all-done.6 = bf16[4,2,64,1280]{3,2,1,0:T(8,128)(2,1)S(1)} async-done(((bf16[4,2,64,1280]{3,2,1,0:T(8,128)(2,1)}), bf16[4,2,64,1280]{3,2,1,0:T(8,128)(2,1)S(1)}, u32[]{:S(2)}, u32[]{:S(2)}) %all-to-all-start.6) | async-done | bytes 1310752 | tf_op jit(solution)/shard_map/all_to_all | solution.py:179
  362.1 7.9 %all-to-all-done.8 = bf16[4,3,40,640]{3,2,1,0:T(8,128)(2,1)S(1)} async-done(((bf16[4,3,40,640]{3,2,1,0:T(8,128)(2,1)}), bf16[4,3,40,640]{3,2,1,0:T(8,128)(2,1)S(1)}, u32[]{:S(2)}, u32[]{:S(2)}) %all-to-all-start.8) | async-done | bytes 614432 | tf_op jit(solution)/shard_map/all_to_all | solution.py:94
  371.9 5.6 %all-to-all-start.9 = ((f32[32,3,640]{2,1,0:T(4,128)}), f32[32,3,640]{2,1,0:T(4,128)}, u32[]{:S(2)}, u32[]{:S(2)}) async-start(f32[32,3,640]{2,1,0:T(4,128)} %broadcast_in_dim.25), calls=%async_computation.9 | async-start | bytes 655360 | tf_op jit(solution)/shard_map/all_to_all | solution.py:33
  382.7 5.8 %all-to-all-done.9 = f32[32,3,640]{2,1,0:T(4,128)} async-done(((f32[32,3,640]{2,1,0:T(4,128)}), f32[32,3,640]{2,1,0:T(4,128)}, u32[]{:S(2)}, u32[]{:S(2)}) %all-to-all-start.9) | async-done | bytes 245792 | tf_op jit(solution)/shard_map/all_to_all | solution.py:33
  (183 shorter events, 139.3 us)
Async XLA Ops:
  2.1 6.7 %collective-permute-start.4 = (bf16[3,20,640]{2,1,0:T(8,128)(2,1)S(1)}, bf16[3,20,640]{2,1,0:T(8,128)(2,1)S(1)}, u32[]{:S(2)}, u32[]{:S(2)}) collective-permute-start(bf16[3,20,640]{2,1,0:T(8,128)(2,1)S(1)} %bitcast.172), channel_id=1, source_target_pairs={{0,16},{16,0},{1,17},{17,1},{2,18},{18,2},{3,19},{19,3},{4,20},{20... | collective-permute-start | bytes 230408 | tf_op jit(solution)/shard_map/ppermute | solution.py:28
  25.2 71.4 %all-to-all-start.1 = ((bf16[4,4,3,40,640]{4,3,2,1,0:T(8,128)(2,1)}), bf16[4,4,3,40,640]{4,3,2,1,0:T(8,128)(2,1)S(1)}, u32[]{:S(2)}, u32[]{:S(2)}) async-start(bf16[4,4,3,40,640]{4,3,2,1,0:T(8,128)(2,1)} %broadcast_in_dim.22), calls=%async_computation.1 | async-start | bytes 4915200 | tf_op jit(solution)/shard_map/all_to_all | solution.py:33
  32.0 64.9 %collective-permute-start.7 = (bf16[256,640]{1,0:T(8,128)(2,1)}, bf16[256,640]{1,0:T(8,128)(2,1)}, u32[]{:S(2)}, u32[]{:S(2)}) collective-permute-start(bf16[256,640]{1,0:T(8,128)(2,1)} %get-tuple-element.56), channel_id=1, source_target_pairs={{0,16},{16,0},{1,17},{17,1},{2,18},{18,2},{3,19},{19,3},{4,20},{20... | collective-permute-start | bytes 983048 | tf_op jit(solution)/shard_map/ppermute | solution.py:28
  34.8 9.6 %collective-permute-start.5 = (f32[256,3]{0,1:T(4,128)S(1)}, f32[256,3]{0,1:T(4,128)S(1)}, u32[]{:S(2)}, u32[]{:S(2)}) collective-permute-start(f32[256,3]{0,1:T(4,128)S(1)} %get-tuple-element.87), channel_id=1, source_target_pairs={{0,16},{16,0},{1,17},{17,1},{2,18},{18,2},{3,19},{19,3},{4,20},{20... | collective-permute-start | bytes 9224 | tf_op jit(solution)/shard_map/ppermute | solution.py:28
  35.6 15.8 %collective-permute-start.8 = (bf16[256,640]{1,0:T(8,128)(2,1)S(1)}, bf16[256,640]{1,0:T(8,128)(2,1)S(1)}, u32[]{:S(2)}, u32[]{:S(2)}) collective-permute-start(bf16[256,640]{1,0:T(8,128)(2,1)S(1)} %get-tuple-element.57), channel_id=1, source_target_pairs={{0,16},{16,0},{1,17},{17,1},{2,18},{18,2},{3,19},{19,3},{4,20},{20... | collective-permute-start | bytes 983048 | tf_op jit(solution)/shard_map/ppermute | solution.py:28
  39.6 61.7 %collective-permute-start.6 = (bf16[256,640]{1,0:T(8,128)(2,1)}, bf16[256,640]{1,0:T(8,128)(2,1)}, u32[]{:S(2)}, u32[]{:S(2)}) collective-permute-start(bf16[256,640]{1,0:T(8,128)(2,1)} %get-tuple-element.61), channel_id=1, source_target_pairs={{0,16},{16,0},{1,17},{17,1},{2,18},{18,2},{3,19},{19,3},{4,20},{20... | collective-permute-start | bytes 983048 | tf_op jit(solution)/shard_map/ppermute | solution.py:28
  40.3 50.2 %collective-permute-start = (bf16[256,640]{1,0:T(8,128)(2,1)}, bf16[256,640]{1,0:T(8,128)(2,1)}, u32[]{:S(2)}, u32[]{:S(2)}) collective-permute-start(bf16[256,640]{1,0:T(8,128)(2,1)} %get-tuple-element.59), channel_id=1, source_target_pairs={{0,16},{16,0},{1,17},{17,1},{2,18},{18,2},{3,19},{19,3},{4,20},{20... | collective-permute-start | bytes 983048 | tf_op jit(solution)/shard_map/ppermute | solution.py:28
  59.0 58.6 %collective-permute-start.9 = (bf16[2,256,1280]{2,1,0:T(8,128)(2,1)}, bf16[2,256,1280]{2,1,0:T(8,128)(2,1)}, u32[]{:S(2)}, u32[]{:S(2)}) collective-permute-start(bf16[2,256,1280]{2,1,0:T(8,128)(2,1)} %broadcast_add_fusion.2), channel_id=1, source_target_pairs={{0,4},{4,8},{8,12},{12,16},{16,20},{20,24},{24,28},{28,32},{32,36}... | collective-permute-start | bytes 3932168 | tf_op jit(solution)/shard_map/ppermute | solution.py:51
  110.6 42.8 %all-to-all-start.2 = ((bf16[4,4,3,40,640]{4,3,1,2,0:T(8,128)(2,1)}), bf16[4,4,3,40,640]{4,3,1,2,0:T(8,128)(2,1)}, u32[]{:S(2)}, u32[]{:S(2)}) async-start(bf16[4,4,3,40,640]{4,3,1,2,0:T(8,128)(2,1)} %pad_maximum_fusion), calls=%async_computation.2 | async-start | bytes 4915200 | tf_op jit(solution)/shard_map/all_to_all | solution.py:90
  117.6 30.0 %collective-permute-start.1 = (bf16[2,256,1280]{2,1,0:T(8,128)(2,1)}, bf16[2,256,1280]{2,1,0:T(8,128)(2,1)}, u32[]{:S(2)}, u32[]{:S(2)}) collective-permute-start(bf16[2,256,1280]{2,1,0:T(8,128)(2,1)} %broadcast_add_fusion.4), channel_id=1, source_target_pairs={{0,4},{4,8},{8,12},{12,16},{16,20},{20,24},{24,28},{28,32},{32,36}... | collective-permute-start | bytes 3932168 | tf_op jit(solution)/shard_map/ppermute | solution.py:51
  168.8 15.3 %all-to-all-start.4 = ((bf16[4,3,40,640]{3,2,1,0:T(8,128)(2,1)}), bf16[4,3,40,640]{3,2,1,0:T(8,128)(2,1)S(1)}, u32[]{:S(2)}, u32[]{:S(2)}) async-start(bf16[4,3,40,640]{3,2,1,0:T(8,128)(2,1)} %broadcast_in_dim.23), calls=%async_computation.4 | async-start | bytes 1228800 | tf_op jit(solution)/shard_map/all_to_all | solution.py:33
  185.8 34.3 %all-to-all-start.5 = ((bf16[4,4,3,40,640]{4,3,2,1,0:T(8,128)(2,1)}), bf16[4,4,3,40,640]{4,3,2,1,0:T(8,128)(2,1)}, u32[]{:S(2)}, u32[]{:S(2)}) async-start(bf16[4,4,3,40,640]{4,3,2,1,0:T(8,128)(2,1)} %broadcast_in_dim.24), calls=%async_computation.5 | async-start | bytes 4915200 | tf_op jit(solution)/shard_map/all_to_all | solution.py:33
  192.9 58.2 %collective-permute-start.2 = (bf16[256,640]{1,0:T(8,128)(2,1)}, bf16[256,640]{1,0:T(8,128)(2,1)}, u32[]{:S(2)}, u32[]{:S(2)}) collective-permute-start(bf16[256,640]{1,0:T(8,128)(2,1)} %get-tuple-element.51), channel_id=1, source_target_pairs={{0,16},{16,0},{1,17},{17,1},{2,18},{18,2},{3,19},{19,3},{4,20},{20... | collective-permute-start | bytes 983048 | tf_op jit(solution)/shard_map/ppermute | solution.py:28
  192.9 67.6 %collective-permute-start.10 = (bf16[256,640]{1,0:T(8,128)(2,1)}, bf16[256,640]{1,0:T(8,128)(2,1)}, u32[]{:S(2)}, u32[]{:S(2)}) collective-permute-start(bf16[256,640]{1,0:T(8,128)(2,1)} %get-tuple-element.53), channel_id=1, source_target_pairs={{0,16},{16,0},{1,17},{17,1},{2,18},{18,2},{3,19},{19,3},{4,20},{20... | collective-permute-start | bytes 983048 | tf_op jit(solution)/shard_map/ppermute | solution.py:28
  202.2 108.4 %collective-permute-start.12 = (bf16[2,256,1280]{2,1,0:T(8,128)(2,1)}, bf16[2,256,1280]{2,1,0:T(8,128)(2,1)}, u32[]{:S(2)}, u32[]{:S(2)}) collective-permute-start(bf16[2,256,1280]{2,1,0:T(8,128)(2,1)} %broadcast_add_fusion.1), channel_id=1, source_target_pairs={{0,4},{4,8},{8,12},{12,16},{16,20},{20,24},{24,28},{28,32},{32,36}... | collective-permute-start | bytes 3932168 | tf_op jit(solution)/shard_map/ppermute | solution.py:51
  204.7 105.9 %collective-permute-start.13 = (bf16[2,256,1280]{2,1,0:T(8,128)(2,1)}, bf16[2,256,1280]{2,1,0:T(8,128)(2,1)}, u32[]{:S(2)}, u32[]{:S(2)}) collective-permute-start(bf16[2,256,1280]{2,1,0:T(8,128)(2,1)} %broadcast_add_fusion), channel_id=1, source_target_pairs={{0,4},{4,8},{8,12},{12,16},{16,20},{20,24},{24,28},{28,32},{32,36}... | collective-permute-start | bytes 3932168 | tf_op jit(solution)/shard_map/ppermute | solution.py:51
  236.8 97.2 %all-to-all-start.7 = ((bf16[4,4,3,40,640]{4,3,1,2,0:T(8,128)(2,1)}), bf16[4,4,3,40,640]{4,3,1,2,0:T(8,128)(2,1)S(1)}, u32[]{:S(2)}, u32[]{:S(2)}) async-start(bf16[4,4,3,40,640]{4,3,1,2,0:T(8,128)(2,1)} %pad_maximum_fusion.2), calls=%async_computation.7 | async-start | bytes 4915200 | tf_op jit(solution)/shard_map/all_to_all | solution.py:90
  271.1 60.1 %collective-permute-start.11 = (bf16[2,256,640]{2,1,0:T(8,128)(2,1)}, bf16[2,256,640]{2,1,0:T(8,128)(2,1)S(1)}, u32[]{:S(2)}, u32[]{:S(2)}) collective-permute-start(bf16[2,256,640]{2,1,0:T(8,128)(2,1)} %pad_maximum_fusion.8), channel_id=1, source_target_pairs={{0,16},{16,0},{1,17},{17,1},{2,18},{18,2},{3,19},{19,3},{4,20},{20... | collective-permute-start | bytes 1966088 | tf_op jit(solution)/shard_map/ppermute | solution.py:28
  335.4 20.9 %all-to-all-start.6 = ((bf16[4,2,64,1280]{3,2,1,0:T(8,128)(2,1)}), bf16[4,2,64,1280]{3,2,1,0:T(8,128)(2,1)S(1)}, u32[]{:S(2)}, u32[]{:S(2)}) async-start(bf16[4,2,64,1280]{3,2,1,0:T(8,128)(2,1)} %bitcast.148), calls=%async_computation.6 | async-start | bytes 2621440 | tf_op jit(solution)/shard_map/all_to_all | solution.py:179
  338.9 50.6 %collective-permute-start.16 = (f32[3,640]{1,0:T(4,128)S(1)}, f32[3,640]{1,0:T(4,128)S(1)}, u32[]{:S(2)}, u32[]{:S(2)}) collective-permute-start(f32[3,640]{1,0:T(4,128)S(1)} %get-tuple-element.76), channel_id=1, source_target_pairs={{0,16},{16,0},{1,17},{17,1},{2,18},{18,2},{3,19},{19,3},{4,20},{20... | collective-permute-start | bytes 23048 | tf_op jit(solution)/shard_map/ppermute | solution.py:28
  356.2 13.8 %all-to-all-start.8 = ((bf16[4,3,40,640]{3,2,1,0:T(8,128)(2,1)}), bf16[4,3,40,640]{3,2,1,0:T(8,128)(2,1)S(1)}, u32[]{:S(2)}, u32[]{:S(2)}) async-start(bf16[4,3,40,640]{3,2,1,0:T(8,128)(2,1)} %copy.245), calls=%async_computation.8 | async-start | bytes 1228800 | tf_op jit(solution)/shard_map/all_to_all | solution.py:94
  371.9 16.6 %all-to-all-start.9 = ((f32[32,3,640]{2,1,0:T(4,128)}), f32[32,3,640]{2,1,0:T(4,128)}, u32[]{:S(2)}, u32[]{:S(2)}) async-start(f32[32,3,640]{2,1,0:T(4,128)} %broadcast_in_dim.25), calls=%async_computation.9 | async-start | bytes 655360 | tf_op jit(solution)/shard_map/all_to_all | solution.py:33
  378.9 11.1 %collective-permute-start.14 = (f32[3,20,640]{2,1,0:T(8,128)S(1)}, f32[3,20,640]{2,1,0:T(8,128)S(1)}, u32[]{:S(2)}, u32[]{:S(2)}) collective-permute-start(f32[3,20,640]{2,1,0:T(8,128)S(1)} %slice.215), channel_id=1, source_target_pairs={{0,16},{16,0},{1,17},{17,1},{2,18},{18,2},{3,19},{19,3},{4,20},{20... | collective-permute-start | bytes 460808 | tf_op jit(solution)/shard_map/ppermute | solution.py:28
  382.3 10.2 %collective-permute-start.15 = (f32[3,20,640]{2,1,0:T(8,128)S(1)}, f32[3,20,640]{2,1,0:T(8,128)S(1)}, u32[]{:S(2)}, u32[]{:S(2)}) collective-permute-start(f32[3,20,640]{2,1,0:T(8,128)S(1)} %slice.216), channel_id=1, source_target_pairs={{0,16},{16,0},{1,17},{17,1},{2,18},{18,2},{3,19},{19,3},{4,20},{20... | collective-permute-start | bytes 460808 | tf_op jit(solution)/shard_map/ppermute | solution.py:28
  (32 other events, 151.1 us)
